TPU v7x, 8 devices: a whole 2x2x1 slice. The times are simulated.
8 devices in a mesh: frag: 1 (over z), dev2: 2 (over y), dev: 4 (over x, core).
Axes of the slice: x: 2, y: 2, z: 1, core: 2. Of those that a mesh axis runs over, the one named last changes fastest.
Arguments:
- ao_ints: bfloat16 [116, 116, 116, 116], P(('frag', 'dev'), 'dev2')
- c_occ: bfloat16 [116, 15], P('frag')
- c_vir: bfloat16 [116, 96], P('frag')
Outputs:
- output: float32 [15, 96, 1440], P(None, None, ('frag', 'dev2', 'dev'))
All inputs are finite; a program needn't handle non-finite values.
Results may differ from a plain program's by a relative error of at most 0.001.
Values are sent between devices in bfloat16 or wider.
A program may use at most 1 GiB of HBM per device.

v0:
```python
import jax
import jax.numpy as jnp
from jax import lax
from jax.sharding import PartitionSpec as P


def solution(mesh):
    def local_program(ints_blk, c_occ, c_vir):
        rows_p = ints_blk.shape[0]
        rows_q = ints_blk.shape[1]
        n_occ = c_occ.shape[1]
        n_virt = c_vir.shape[1]
        t_one = jnp.einsum('pqrs,rj->pqsj', ints_blk, c_occ, preferred_element_type=jnp.float32).astype(jnp.bfloat16)
        half_ints = jnp.einsum('pqsj,sb->pqjb', t_one, c_vir, preferred_element_type=jnp.float32).astype(jnp.bfloat16)
        half_ints = half_ints.reshape(rows_p, rows_q, n_occ * n_virt)
        half_ints = lax.all_to_all(half_ints, 'dev2', 2, 1, tiled=True)
        half_ints = lax.all_to_all(half_ints, 'dev', 2, 0, tiled=True)
        g_mid = jnp.einsum('qa,pqc->apc', c_vir, half_ints, preferred_element_type=jnp.float32)
        return jnp.einsum('pi,apc->iac', c_occ.astype(jnp.float32), g_mid, precision=lax.Precision.HIGHEST)

    return jax.shard_map(
        local_program,
        mesh=mesh,
        in_specs=(P(('frag', 'dev'), 'dev2', None, None), P('frag', None), P('frag', None)),
        out_specs=P(None, None, ('frag', 'dev2', 'dev')),
        check_vma=False,
    )
```

profile of v0, /device:TPU:0, one launch (start us, length us, event | category | flops | bytes accessed | tf_op | source)
XLA Modules:
  0.0 290.6 jit_solution(12415656685937839990)
XLA Ops:
  0.0 0.0 copy-start
  0.0 21.5 %convolution_convert_fusion = bf16[29,58,116,15]{2,3,1,0:T(8,128)(2,1)} fusion(bf16[29,58,116,116]{3,2,1,0:T(8,128)(2,1)} %param.3, bf16[116,15]{0,1:T(8,128)(2,1)} %param.4), kind=kOutput, calls=%fused_computation.4 | convolution fusion | flops 681916416 | bytes 51122824 | tf_op jit(solution)/shard_map/pqrs,rj->pqsj/dot_general | solution.py:13
  21.6 0.0 copy-done
  21.6 7.9 %fusion.4 = bf16[29,58,15,96]{3,1,2,0:T(8,128)(2,1)} fusion(bf16[29,58,116,15]{2,3,1,0:T(8,128)(2,1)} %convolution_convert_fusion, bf16[116,96]{0,1:T(8,128)(2,1)S(1)} %copy-done), kind=kOutput, calls=%fused_computation.5 | convolution fusion | flops 564344640 | bytes 10719792 | tf_op jit(solution)/shard_map/pqsj,sb->pqjb/dot_general | solution.py:14
  29.4 20.0 %copy.21 = bf16[29,58,15,96]{1,0,3,2:T(8,128)(2,1)} copy(bf16[29,58,15,96]{3,1,2,0:T(8,128)(2,1)} %fusion.4) | data formatting | bytes 9688320 | tf_op jit(solution)/shard_map/reshape | solution.py:15
  49.5 29.5 %reshape.8 = bf16[2,2,605520]{2,1,0:T(2,128)(2,1)} reshape(bf16[1440,29,58]{2,1,0:T(8,128)(2,1)} %bitcast.34) | data formatting | bytes 9688320
  79.0 64.1 %all_to_all.36 = bf16[2,2,605520]{2,1,0:T(2,128)(2,1)} all-to-all(bf16[2,2,605520]{2,1,0:T(2,128)(2,1)} %reshape.8), channel_id=1, replica_groups=mesh['frag'=1,'dev2'=2,'dev'=4] {'dev2'}, dimensions={0} | all-to-all | bytes 9688320 | tf_op jit(solution)/shard_map/all_to_all | solution.py:16
  143.0 25.9 %reshape.9 = bf16[1440,29,58]{2,1,0:T(8,128)(2,1)} reshape(bf16[2,2,605520]{2,1,0:T(2,128)(2,1)} %all_to_all.36) | data formatting | bytes 9688320
  168.9 17.6 %copy.13 = bf16[29,58,2,720]{3,1,2,0:T(8,128)(2,1)} copy(bf16[29,58,2,720]{1,0,3,2:T(8,128)(2,1)} %bitcast.35) | data formatting | bytes 9688320 | tf_op jit(solution)/shard_map/all_to_all | solution.py:16
  186.5 9.0 %all_to_all.29 = bf16[29,116,720]{2,1,0:T(8,128)(2,1)} reshape(bf16[29,2,58,720]{3,2,1,0:T(8,128)(2,1)} %bitcast.37) | data formatting | bytes 9688320 | tf_op jit(solution)/shard_map/all_to_all | solution.py:16
  195.5 8.8 %copy.14 = bf16[29,116,720]{1,0,2:T(8,128)(2,1)} copy(bf16[29,116,720]{2,1,0:T(8,128)(2,1)} %all_to_all.29) | data formatting | bytes 9688320 | tf_op jit(solution)/shard_map/all_to_all | solution.py:16
  204.3 70.3 %all_to_all.37 = bf16[29,116,720]{1,0,2:T(8,128)(2,1)S(1)} all-to-all(bf16[29,116,720]{1,0,2:T(8,128)(2,1)} %copy.14), channel_id=1, replica_groups=mesh['frag'=1,'dev2'=2,'dev'=4] {'dev'}, dimensions={2} | all-to-all | bytes 9688320 | tf_op jit(solution)/shard_map/all_to_all | solution.py:17
  274.6 2.1 copy.16
  276.8 0.0 copy-start.1
  276.8 3.7 %fusion.7 = f32[116,180,96]{0,2,1:T(8,128)S(1)} fusion(bf16[116,116,180]{1,2,0:T(8,128)(2,1)S(1)} %bitcast.38, bf16[116,96]{0,1:T(8,128)(2,1)S(1)} %copy-done), kind=kOutput, calls=%fused_computation.6 | convolution fusion | flops 465039360 | bytes 12884352 | tf_op jit(solution)/shard_map/qa,pqc->apc/dot_general | solution.py:18
  280.5 0.0 copy-done.1
  280.5 8.2 %fusion.9 = f32[15,96,180]{1,0,2:T(8,128)S(1)} fusion(f32[116,180,96]{0,2,1:T(8,128)S(1)} %fusion.7, bf16[116,15]{0,1:T(8,128)(2,1)S(1)} %copy-done.1), kind=kOutput, calls=%fused_computation.8 | convolution fusion | flops 360806400 | bytes 9058200 | tf_op jit(solution)/shard_map/pi,apc->iac/dot_general | solution.py:19
  288.7 1.5 copy.18
Async XLA Ops:
  0.0 21.6 %copy-start = (bf16[116,96]{0,1:T(8,128)(2,1)S(1)}, bf16[116,96]{0,1:T(8,128)(2,1)}, u32[]{:S(2)}) copy-start(bf16[116,96]{0,1:T(8,128)(2,1)} %param.5) | copy-start | bytes 66820
  276.8 3.7 %copy-start.1 = (bf16[116,15]{0,1:T(8,128)(2,1)S(1)}, bf16[116,15]{0,1:T(8,128)(2,1)}, u32[]{:S(2)}) copy-start(bf16[116,15]{0,1:T(8,128)(2,1)} %param.4) | copy-start | bytes 10444
where the time goes:
time: 296 us; the launch traced here: 291 us
  blocking collectives  134 us (45%)
  local copies, waits for them, and re-layouts  114 us (39%)
  matrix products  41.3 us (14%)
    all_to_all x1, blocking collectives, local_program(): half_ints = lax.all_to_all(half_ints, 'dev', 2, 0, tiled=True)  70.3 us
    all_to_all x1, blocking collectives, local_program(): half_ints = lax.all_to_all(half_ints, 'dev2', 2, 1, tiled=True)  64.1 us
    unnamed x6, local copies, waits for them, and re-layouts  55.4 us
    all_to_all x3, local copies, waits for them, and re-layouts, local_program(): half_ints = lax.all_to_all(half_ints, 'dev2', 2, 1, tiled=True)  35.4 us
    dot_general x1, matrix products, local_program(): jnp.einsum('pqrs,rj->pqsj', ints_blk, c_occ, preferred_element_type=jnp.f...  21.5 us
    reshape x1, local copies, waits for them, and re-layouts, local_program(): half_ints = half_ints.reshape(rows_p, rows_q, n_occ * n_virt)  20 us
    dot_general x1, matrix products, local_program(): jnp.einsum('pi,apc->iac', c_occ.astype(jnp.float32), g_mid, precision=lax...  8.17 us
    dot_general x1, matrix products, local_program(): jnp.einsum('pqsj,sb->pqjb', t_one, c_vir, preferred_element_type=jnp.floa...  7.88 us

commit v1 on v0

v1 whole, which is shorter than its diff:
```python
import functools

import jax
import jax.numpy as jnp
from jax import lax
from jax.experimental import pallas as pl
from jax.experimental.pallas import tpu as pltpu
from jax.sharding import PartitionSpec as P

MESH = pl.DeviceIdType.MESH
F32, BF16, I32 = jnp.float32, jnp.bfloat16, jnp.int32

NP, NQ, NB = 29, 58, 116
NO, NV = 15, 96
QC = 8
NM = NQ // QC
QT = NQ - NM * QC
PG = 4
LW = 384
JR = [((360 * d) // 96, (360 * d + 359) // 96) for d in range(4)]
JO = [sum(hi - lo + 1 for lo, hi in JR[:d]) for d in range(5)]
KF = 144


def iota(shape, dim):
    return lax.broadcasted_iota(I32, shape, dim)


def dot(a, b):
    return jnp.dot(a, b, preferred_element_type=F32)


def kernel(a_hbm, cot_ref, cvt_ref, out_ref, abuf, atail, cot, cvt, s_mat, b_mat, l_mat, lt_mat, g_mat, x_buf,
           own_m, own_t, ps_m, ps_t, pr_m, pr_t, rb_m, rb_t, vsend,
           a_sem, at_sem, d_send, d_recv, r_send, r_recv, v_send, v_recv):
    y = lax.axis_index('dev2')
    dev = lax.axis_index('dev')
    core = lax.rem(dev, 2)
    x = dev // 2
    partner = (0, y, x * 2 + (1 - core))
    peers = [(0, y, (1 - x) * 2 + core), (0, 1 - y, x * 2 + core), (0, 1 - y, (1 - x) * 2 + core)]
    chip = [2 * y + (1 - x), 2 * (1 - y) + x, 2 * (1 - y) + (1 - x)]
    me = 2 * y + x

    def a_copy(n, slot):
        return pltpu.make_async_copy(a_hbm.at[:, pl.ds(n * QC, QC)], abuf.at[slot], a_sem.at[slot])

    tail_copy = pltpu.make_async_copy(a_hbm.at[:, pl.ds(NM * QC, QT)], atail, at_sem)
    tail_copy.start()
    a_copy(0, 0).start()
    a_copy(1, 1).start()

    barrier = pltpu.get_barrier_semaphore()
    for other in [partner] + peers:
        pl.semaphore_signal(barrier, inc=1, device_id=other, device_id_type=MESH)

    cot[...] = jnp.zeros_like(cot)
    cot[0:NO, 0:NB] = cot_ref[...].astype(F32)
    cvt[...] = jnp.zeros_like(cvt)
    cvt[0:NV, 0:NB] = cvt_ref[...].astype(F32)
    sub = iota((8, 128), 0)
    zero = jnp.zeros((8, 128), F32)
    for jj in range(8):
        for p in range(8):
            two = [jnp.where(sub == p, cot[j:j + 1, :], zero) for j in (2 * jj, 2 * jj + 1)]
            s_mat[16 * jj:16 * jj + 16, 128 * p:128 * p + 128] = jnp.concatenate(two, axis=0).astype(BF16)
    cv = cvt[...].T.astype(BF16)
    lane = iota((128, LW), 1)
    rel = jnp.where(lane < 180, lane, jnp.where(lane >= 256, lane - 76, lane + 116))
    bad = ((lane >= 180) & (lane < 192)) | ((lane >= 244) & (lane < 256))
    want = jnp.where(bad, -100000, rel) - iota((128, LW), 0)
    for d in range(4):
        for j in range(JR[d][0], JR[d][1] + 1):
            place = jnp.where(want == 96 * j - 360 * d, 1.0, 0.0).astype(BF16)
            k = JO[d] + j - JR[d][0]
            b_mat[128 * k:128 * k + 128, :] = dot(cv, place).astype(BF16)
    low, high = cot[0:8, :], cot[8:16, :]
    mine = jnp.concatenate([jnp.where(core == 0, low, high), jnp.where(core == 0, high, low)], axis=0)
    kk = iota((128, 256), 1)
    ploc = ((kk >> 4) & 3) * 8 + (kk & 7)
    pick = (iota((128, 256), 0) == ploc + NP * dev) & (ploc < NP)
    l0 = dot(mine.astype(BF16), jnp.where(pick, 1.0, 0.0).astype(BF16)).astype(BF16)
    row, k2 = iota((128, 256), 0), iota((128, 256), 1)
    e8 = jnp.where((iota((128, 16), 0) >> 3) == iota((128, 16), 1), 1.0, 0.0).astype(BF16)
    l_mat[...] = jnp.where((k2 >> 6) * 2 + ((k2 >> 3) & 1) == (row & 7), dot(e8, l0), 0.0).astype(BF16)
    e2 = jnp.where((iota((32, 16), 0) >> 1) == iota((32, 16), 1), 1.0, 0.0).astype(BF16)
    rowt, kt = iota((32, 256), 0), iota((32, 256), 1)
    lt_mat[...] = jnp.where(((kt >> 3) & 1) == (rowt & 1), dot(e2, l0), 0.0).astype(BF16)
    kf = iota((128, 3 * KF), 1)
    kf = jnp.where(kf >= 2 * KF, kf - 2 * KF, jnp.where(kf >= KF, kf - KF, kf))
    base, other_base = NQ * y, NQ * (1 - y)
    want_q = jnp.where(kf < 56, base + kf, jnp.where(kf < 112, other_base + kf - 56,
                       jnp.where(kf < 128, base + 56 + (kf & 1), other_base + 56 + (kf & 1))))
    sel = jnp.where(iota((128, 3 * KF), 0) == want_q, 1.0, 0.0).astype(BF16)
    g_mat[...] = dot(cvt[0:NV, :].astype(BF16), sel)

    pl.semaphore_wait(barrier, 4)

    def step1(a, q0, qps):
        zl = jnp.zeros((NB, 128 - NB), BF16)
        zs = jnp.zeros((128 - NB, 128), BF16)

        def tile(p, q):
            t = jnp.concatenate([a[p, q], zl], axis=1)
            return jnp.concatenate([t, zs], axis=0)

        for qp in qps:
            for pg in range(PG):
                ps = range(8 * pg, min(NP, 8 * pg + 8))
                rhs = jnp.concatenate(
                    [jnp.concatenate([tile(p, 2 * qp), tile(p, 2 * qp + 1)], axis=1) for p in ps], axis=0)
                t = dot(s_mat[0:8 * NO, 0:128 * len(ps)], rhs)
                r = 64 * qp + 16 * pg
                for j in range(NO):
                    two = jnp.concatenate([t[8 * j:8 * j + 8, 0:128], t[8 * j:8 * j + 8, 128:256]], axis=0)
                    x_buf[r:r + 16, 128 * j:128 * j + 128] = two.astype(BF16)

    def step2(rows, lhs, half, own, send):
        for d in range(4):
            lo, hi = JR[d]
            h = dot(x_buf[0:rows, 128 * lo:128 * hi + 128], b_mat[128 * JO[d]:128 * JO[d + 1], :]).astype(BF16)
            w = dot(lhs, h)
            own[d] = w[0:half]
            send[d] = w[half:2 * half]

    def d2d(n):
        return pltpu.make_async_remote_copy(
            src_ref=ps_m.at[n], dst_ref=pr_m.at[n], send_sem=d_send.at[n], recv_sem=d_recv.at[n],
            device_id=partner, device_id_type=MESH)

    d2d_t = pltpu.make_async_remote_copy(
        src_ref=ps_t, dst_ref=pr_t, send_sem=d_send.at[NM], recv_sem=d_recv.at[NM],
        device_id=partner, device_id_type=MESH)

    def out_m(n, k):
        return pltpu.make_async_remote_copy(
            src_ref=own_m.at[n, chip[k]], dst_ref=rb_m.at[k, n], send_sem=r_send.at[n, k], recv_sem=r_recv.at[n, k],
            device_id=peers[k], device_id_type=MESH)

    def out_t(k):
        return pltpu.make_async_remote_copy(
            src_ref=own_t.at[chip[k]], dst_ref=rb_t.at[k], send_sem=r_send.at[NM, k], recv_sem=r_recv.at[NM, k],
            device_id=peers[k], device_id_type=MESH)

    def finish_m(n):
        d2d(n).wait_recv()
        own_m[n] = own_m[n] + pr_m[n]
        for k in (2, 0, 1):
            out_m(n, k).start()

    def finish_t():
        d2d_t.wait_recv()
        own_t[...] = own_t[...] + pr_t[...]
        for k in (2, 0, 1):
            out_t(k).start()

    tail_copy.wait()
    step1(atail, 0, range(QT // 2))
    step2(64, lt_mat[:, 0:64], 16, own_t, ps_t)
    d2d_t.start()

    def body(n, carry):
        slot = lax.rem(n, 2)
        a_copy(n, slot).wait()
        a = abuf.at[slot]
        step1(a, 0, range(2))

        @pl.when(n == 0)
        def _():
            finish_t()

        @pl.when(n > 0)
        def _():
            finish_m(n - 1)

        step1(a, 0, range(2, 4))

        @pl.when(n + 2 < NM)
        def _():
            a_copy(n + 2, slot).start()

        step2(256, l_mat[...], 64, own_m.at[n], ps_m.at[n])
        d2d(n).start()
        return carry

    lax.fori_loop(0, NM, body, 0)
    finish_m(NM - 1)

    for k in range(3):
        out_t(k).wait_recv()

    def arrive(n, carry):
        for k in range(3):
            out_m(n, k).wait_recv()
        return carry

    lax.fori_loop(0, NM, arrive, 0)

    kg = iota((NV, 3 * KF), 1)
    kg = jnp.where(kg >= 2 * KF, kg - 2 * KF, jnp.where(kg >= KF, kg - KF, kg))
    which = jnp.where(kg < 112, -1, ((kg - 112) & 15) >> 1)

    def back(i):
        return pltpu.make_async_remote_copy(
            src_ref=vsend.at[i], dst_ref=out_ref.at[core * 8 + i], send_sem=v_send.at[i], recv_sem=v_recv.at[i],
            device_id=partner, device_id_type=MESH)

    def back_in(i):
        return pltpu.make_async_remote_copy(
            src_ref=vsend.at[i], dst_ref=out_ref.at[(1 - core) * 8 + i], send_sem=v_send.at[i], recv_sem=v_recv.at[i],
            device_id=partner, device_id_type=MESH)

    tails = [own_t[me] + rb_t[0], rb_t[1] + rb_t[2]]

    def last(i, carry):
        rows = pl.ds(pl.multiple_of(8 * i, 8), 8)
        near = [own_m[n, me, rows, :] + rb_m[0, n, rows, :] for n in range(NM)]
        far = [rb_m[1, n, rows, :] + rb_m[2, n, rows, :] for n in range(NM)]
        w = jnp.concatenate(near + far + tails, axis=0)
        hi = w.astype(BF16)
        r1 = w - hi.astype(F32)
        mid = r1.astype(BF16)
        lo = (r1 - mid.astype(F32)).astype(BF16)
        lhs = jnp.where((which < 0) | (which == i), g_mat[...], 0.0).astype(BF16)
        v = dot(lhs, jnp.concatenate([hi, mid, lo], axis=0))
        c0, c1, c2 = v[:, 0:128], v[:, 128:256], v[:, 256:384]
        c3 = pltpu.roll(c1, 64, 1)
        mine_v = jnp.concatenate([jnp.where(core == 0, c0, c2), jnp.where(core == 0, c1, c3)], axis=1)
        theirs = jnp.concatenate([jnp.where(core == 0, c2, c0), jnp.where(core == 0, c3, c1)], axis=1)
        out_ref[core * 8 + i] = mine_v[:, 0:180]
        vsend[i] = theirs[:, 0:180]
        back(i).start()
        return carry

    lax.fori_loop(0, 8, last, 0)

    def drain_v(i, carry):
        back_in(i).wait_recv()
        back(i).wait_send()
        return carry

    lax.fori_loop(0, 8, drain_v, 0)
    d2d_t.wait_send()
    for k in range(3):
        out_t(k).wait_send()

    def drain(n, carry):
        d2d(n).wait_send()
        for k in range(3):
            out_m(n, k).wait_send()
        return carry

    lax.fori_loop(0, NM, drain, 0)


def solution(mesh):
    def local_program(ints_blk, c_occ, c_vir):
        v = pl.pallas_call(
            kernel,
            out_shape=jax.ShapeDtypeStruct((16, NV, 180), F32),
            in_specs=[pl.BlockSpec(memory_space=pl.ANY),
                      pl.BlockSpec(memory_space=pltpu.VMEM), pl.BlockSpec(memory_space=pltpu.VMEM)],
            out_specs=pl.BlockSpec(memory_space=pltpu.VMEM),
            scratch_shapes=[
                pltpu.VMEM((2, NP, QC, NB, NB), BF16),
                pltpu.VMEM((NP, QT, NB, NB), BF16),
                pltpu.VMEM((16, 128), F32),
                pltpu.VMEM((128, 128), F32),
                pltpu.VMEM((128, 1024), BF16),
                pltpu.VMEM((128 * JO[4], LW), BF16),
                pltpu.VMEM((128, 256), BF16),
                pltpu.VMEM((32, 256), BF16),
                pltpu.VMEM((NV, 3 * KF), F32),
                pltpu.VMEM((256, 128 * NO), BF16),
                pltpu.VMEM((NM, 4, 64, LW), F32),
                pltpu.VMEM((4, 16, LW), F32),
                pltpu.VMEM((NM, 4, 64, LW), F32),
                pltpu.VMEM((4, 16, LW), F32),
                pltpu.VMEM((NM, 4, 64, LW), F32),
                pltpu.VMEM((4, 16, LW), F32),
                pltpu.VMEM((3, NM, 64, LW), F32),
                pltpu.VMEM((3, 16, LW), F32),
                pltpu.VMEM((8, NV, 180), F32),
                pltpu.SemaphoreType.DMA((2,)),
                pltpu.SemaphoreType.DMA,
                pltpu.SemaphoreType.DMA((NM + 1,)),
                pltpu.SemaphoreType.DMA((NM + 1,)),
                pltpu.SemaphoreType.DMA((NM + 1, 3)),
                pltpu.SemaphoreType.DMA((NM + 1, 3)),
                pltpu.SemaphoreType.DMA((8,)),
                pltpu.SemaphoreType.DMA((8,)),
            ],
            compiler_params=pltpu.CompilerParams(
                collective_id=0, has_side_effects=True, vmem_limit_bytes=60 * 1024 * 1024),
            name='four_index',
        )(ints_blk, c_occ.T, c_vir.T)
        return v[0:NO]

    return jax.shard_map(
        local_program,
        mesh=mesh,
        in_specs=(P(('frag', 'dev'), 'dev2', None, None), P('frag', None), P('frag', None)),
        out_specs=P(None, None, ('frag', 'dev2', 'dev')),
        check_vma=False,
    )
```

time: 296 us -> 52.3 us (0.18); the launches traced: 291 us -> 52.1 us
  blocking collectives: 134 us -> 0 us
  local copies, waits for them, and re-layouts: 114 us -> 2.97 us
  Pallas kernels: 0 us -> 49.1 us
  matrix products: 41.3 us -> 0 us
    all_to_all x2 -> x0, blocking collectives: 134 us -> none  [the longest x1 70.3 us: local_program(): half_ints = lax.all_to_all(half_ints, 'dev', 2, 0, tiled=True)]
    unnamed x6 -> x0, local copies, waits for them, and re-layouts: 55.4 us -> none
    pallas_call x0 -> x1, Pallas kernels: none -> 49.1 us  [local_program(): pl.pallas_call(kernel, out_shape=jax.ShapeDtypeStruct((16, NV, 180), F32)...]
    dot_general x4 -> x0, matrix products: 41.3 us -> none  [the longest x1 21.5 us: local_program(): jnp.einsum('pqrs,rj->pqsj', ints_blk, c_occ, preferred_element_type=jnp.f...]
    all_to_all x4 -> x0, local copies, waits for them, and re-layouts: 37.5 us -> none  [the longest x3 35.4 us: local_program(): half_ints = lax.all_to_all(half_ints, 'dev2', 2, 1, tiled=True)]
    reshape x1 -> x0, local copies, waits for them, and re-layouts: 20 us -> none  [local_program(): half_ints = half_ints.reshape(rows_p, rows_q, n_occ * n_virt)]
    slice x0 -> x3, local copies, waits for them, and re-layouts: none -> 2.97 us  [local_program(): return v[0:NO]]
where the time goes in v1:
time: 52.3 us; the launch traced here: 52.1 us
  Pallas kernels  49.1 us (94%)
  local copies, waits for them, and re-layouts  2.97 us (6%)
    pallas_call x1, Pallas kernels, local_program(): pl.pallas_call(kernel, out_shape=jax.ShapeDtypeStruct((16, NV, 180), F32)...  49.1 us
    slice x3, local copies, waits for them, and re-layouts, local_program(): return v[0:NO]  2.97 us

profile of v1, /device:TPU:0, one launch (start us, length us, event | category | flops | bytes accessed | tf_op | source)
XLA Modules:
  0.0 52.1 jit_solution(16303885971198189201)
XLA Ops:
  0.0 49.1 %four_index.1 = f32[16,96,180]{2,1,0:T(8,128)} custom-call(bf16[29,58,116,116]{3,2,1,0:T(8,128)(2,1)} %a_hbm.1, bf16[15,116]{1,0:T(8,128)(2,1)} %bitcast.3, bf16[96,116]{1,0:T(8,128)(2,1)} %bitcast.2), custom_call_target="tpu_custom_call" | custom-call | tf_op jit(solution)/shard_map/four_index/pallas_call | solution.py:258
  49.1 0.0 slice-start
  49.1 1.4 %slice-done = f32[15,96,180]{2,1,0:T(8,128)S(1)} async-done(((f32[16,96,180]{2,1,0:T(8,128)}), f32[15,96,180]{2,1,0:T(8,128)S(1)}, s32[]{:S(2)}) %slice-start) | async-done | bytes 1036824 | tf_op jit(solution)/shard_map/slice | solution.py:297
  50.5 1.6 %copy.4 = f32[15,96,180]{1,2,0:T(8,128)} copy(f32[15,96,180]{2,1,0:T(8,128)S(1)} %slice-done) | data formatting | bytes 2073600 | tf_op jit(solution)/shard_map/slice | solution.py:297
Async XLA Ops:
  49.1 1.4 %slice-start = ((f32[16,96,180]{2,1,0:T(8,128)}), f32[15,96,180]{2,1,0:T(8,128)S(1)}, s32[]{:S(2)}) async-start(f32[16,96,180]{2,1,0:T(8,128)} %four_index.1), calls=%async_computation | async-start | bytes 2949120 | tf_op jit(solution)/shard_map/slice | solution.py:297

commit v2 on v0

v2 whole, which is shorter than its diff:
```python
import jax
import jax.numpy as jnp
from jax import lax
from jax.experimental import pallas as pl
from jax.experimental.pallas import tpu as pltpu
from jax.sharding import PartitionSpec as P

MESH = pl.DeviceIdType.MESH
F32, BF16, I32 = jnp.float32, jnp.bfloat16, jnp.int32

NP, NQ, NB = 29, 58, 116
NO, NV = 15, 96
QC = 8
NM = NQ // QC
QT = NQ - NM * QC
PG = 4
LW = 384
NJ = 5
RW = 184
ROWS = (RW, RW - 24)
N1 = 4
K1, K2 = 16 * N1 + 32, 16 * (NM - N1)


def iota(shape, dim):
    return lax.broadcasted_iota(I32, shape, dim)


def dot(a, b):
    return jnp.dot(a, b, preferred_element_type=F32)


def parts(w):
    hi = w.astype(BF16)
    rest = w - hi.astype(F32)
    mid = rest.astype(BF16)
    lo = (rest - mid.astype(F32)).astype(BF16)
    return jnp.concatenate([hi, mid, lo], axis=0)


def kernel(a_hbm, cot_hbm, cvt_hbm, out_hbm, abuf, atail, cot_in, cvt_in, cot, cvt, s_mat, b_mat, l_mat, lt_mat,
           g1_mat, g2_mat, x_buf, own_m, own_t, ps_m, ps_t, pr_m, pr_t, rb_m, rb_t, v_acc, v_own, v_other,
           a_sem, at_sem, c_sem, d_send, d_recv, r_send, r_recv, v_send, v_recv, o_sem):
    y = lax.axis_index('dev2')
    dev = lax.axis_index('dev')
    core = lax.rem(dev, 2)
    x = dev // 2
    partner = (0, y, x * 2 + (1 - core))
    peers = [(0, 1 - y, (1 - x) * 2 + core), (0, y, (1 - x) * 2 + core), (0, 1 - y, x * 2 + core)]
    chip = [2 * (1 - y) + (1 - x), 2 * y + (1 - x), 2 * (1 - y) + x, 2 * y + x]

    def a_copy(n, qp, slot):
        return pltpu.make_async_copy(
            a_hbm.at[:, pl.ds(n * QC + 2 * qp, 2)], abuf.at[slot, qp], a_sem.at[slot, qp])

    small = [pltpu.make_async_copy(cot_hbm, cot_in, c_sem.at[0]), pltpu.make_async_copy(cvt_hbm, cvt_in, c_sem.at[1])]
    tail_copy = pltpu.make_async_copy(a_hbm.at[:, pl.ds(NM * QC, QT)], atail, at_sem)
    for c in small:
        c.start()
    tail_copy.start()

    barrier = pltpu.get_barrier_semaphore()
    for other in [partner] + peers:
        pl.semaphore_signal(barrier, inc=1, device_id=other, device_id_type=MESH)

    cot[...] = jnp.zeros_like(cot)
    cvt[...] = jnp.zeros_like(cvt)
    for c in small:
        c.wait()
    cot[0:NO, 0:NB] = cot_in[...].astype(F32)
    cvt[0:NV, 0:NB] = cvt_in[...].astype(F32)
    for qp in range(4):
        a_copy(0, qp, 0).start()
    sub = iota((8, 128), 0)
    zero = jnp.zeros((8, 128), F32)
    for jj in range(8):
        for p in range(8):
            two = [jnp.where(sub == p, cot[j:j + 1, :], zero) for j in (2 * jj, 2 * jj + 1)]
            s_mat[16 * jj:16 * jj + 16, 128 * p:128 * p + 128] = jnp.concatenate(two, axis=0).astype(BF16)
    cv = cvt[...].T.astype(BF16)
    lane = iota((128, LW), 1)
    rel = jnp.where(lane < 128, lane, jnp.where(lane < 256, lane + 52, jnp.where(lane < 308, lane - 128, lane)))
    want = jnp.where(lane >= 360, -100000, rel) - iota((128, LW), 0)
    for d in range(4):
        for j in range(NJ):
            place = jnp.where(want == 96 * ((7 * d) // 2 + j) - 360 * d, 1.0, 0.0).astype(BF16)
            b_mat[d, 128 * j:128 * j + 128, :] = dot(cv, place).astype(BF16)
    low, high = cot[0:8, :], cot[8:16, :]
    mine = jnp.concatenate([jnp.where(core == 0, low, high), jnp.where(core == 0, high, low)], axis=0)
    kk = iota((128, 256), 1)
    ploc = ((kk >> 4) & 3) * 8 + (kk & 7)
    pick = (iota((128, 256), 0) == ploc + NP * dev) & (ploc < NP)
    l0 = dot(mine.astype(BF16), jnp.where(pick, 1.0, 0.0).astype(BF16)).astype(BF16)
    row, k2 = iota((128, 256), 0), iota((128, 256), 1)
    e8 = jnp.where((iota((128, 16), 0) >> 3) == iota((128, 16), 1), 1.0, 0.0).astype(BF16)
    l_mat[...] = jnp.where((k2 >> 6) * 2 + ((k2 >> 3) & 1) == (row & 7), dot(e8, l0), 0.0).astype(BF16)
    e2 = jnp.where((iota((32, 16), 0) >> 1) == iota((32, 16), 1), 1.0, 0.0).astype(BF16)
    rowt, kt = iota((32, 256), 0), iota((32, 256), 1)
    lt_mat[...] = jnp.where(((kt >> 3) & 1) == (rowt & 1), dot(e2, l0), 0.0).astype(BF16)

    base, other_base = NQ * y, NQ * (1 - y)

    def fold(k, period):
        return jnp.where(k >= 2 * period, k - 2 * period, jnp.where(k >= period, k - period, k))

    def g_of(k, want_q):
        sel = jnp.where(iota((128, k), 0) == want_q, 1.0, 0.0).astype(BF16)
        return dot(cvt[0:NV, :].astype(BF16), sel)

    k1 = fold(iota((128, 3 * K1), 1), K1)
    h1 = 8 * N1
    want1 = jnp.where(k1 < h1, base + k1, jnp.where(k1 < 2 * h1, other_base + k1 - h1,
                      jnp.where(k1 < 2 * h1 + 16, base, other_base) + NM * QC + (k1 & 1)))
    g1_mat[...] = g_of(3 * K1, want1)
    k2f = fold(iota((128, 3 * K2), 1), K2)
    h2 = 8 * (NM - N1)
    g2_mat[...] = g_of(3 * K2, jnp.where(k2f < h2, base + h1 + k2f, other_base + h1 + k2f - h2)).astype(BF16)

    def step1(tile_of, qp):
        zl = jnp.zeros((NB, 128 - NB), BF16)
        zs = jnp.zeros((128 - NB, 128), BF16)

        def tile(p, q):
            t = jnp.concatenate([tile_of(p, q), zl], axis=1)
            return jnp.concatenate([t, zs], axis=0)

        for pg in range(PG):
            ps = range(8 * pg, min(NP, 8 * pg + 8))
            rhs = jnp.concatenate([jnp.concatenate([tile(p, 0), tile(p, 1)], axis=1) for p in ps], axis=0)
            t = dot(s_mat[0:8 * NO, 0:128 * len(ps)], rhs)
            r = 64 * qp + 16 * pg
            for j in range(NO):
                two = jnp.concatenate([t[8 * j:8 * j + 8, 0:128], t[8 * j:8 * j + 8, 128:256]], axis=0)
                x_buf[j, r:r + 16, :] = two.astype(BF16)

    def step2(rows, lhs, r):
        first = (7 * chip[r]) // 2
        t = jnp.concatenate([x_buf[first + j, 0:rows, :] for j in range(NJ)], axis=1)
        return dot(lhs, dot(t, b_mat[chip[r]]).astype(BF16))

    spare = iota((8, 128), 1) >= 104

    def pack(ref, w):
        col = [[w[8 * i:8 * i + 8, 128 * c:128 * c + 128] for c in range(3)] for i in range(8)]
        ref[0:8, :] = col[0][0]
        ref[8:16, :] = col[0][1]
        for i in range(1, 8):
            third = col[i][2]
            if i <= 5:
                third = jnp.where(spare, pltpu.roll(col[0][2], 104 - 24 * (i - 1), 1), third)
            b = 24 * i - 8
            ref[b:b + 8, :] = col[i][0]
            ref[b + 8:b + 16, :] = col[i][1]
            ref[b + 16:b + 24, :] = third

    def d2d(n, r):
        return pltpu.make_async_remote_copy(
            src_ref=ps_m.at[n, r], dst_ref=pr_m.at[n, r], send_sem=d_send.at[n, r], recv_sem=d_recv.at[n, r],
            device_id=partner, device_id_type=MESH)

    def d2d_t(r):
        return pltpu.make_async_remote_copy(
            src_ref=ps_t.at[r], dst_ref=pr_t.at[r], send_sem=d_send.at[NM, r], recv_sem=d_recv.at[NM, r],
            device_id=partner, device_id_type=MESH)

    def out_m(n, r, rows):
        return pltpu.make_async_remote_copy(
            src_ref=own_m.at[n, r, pl.ds(0, rows)], dst_ref=rb_m.at[r, n, pl.ds(0, rows)],
            send_sem=r_send.at[n, r], recv_sem=r_recv.at[n, r], device_id=peers[r], device_id_type=MESH)

    def out_t(r):
        return pltpu.make_async_remote_copy(
            src_ref=own_t.at[r], dst_ref=rb_t.at[r], send_sem=r_send.at[NM, r], recv_sem=r_recv.at[NM, r],
            device_id=peers[r], device_id_type=MESH)

    def by_core(f):
        for k in range(2):
            @pl.when(core == k)
            def _(k=k):
                f(ROWS[k])

    def finish_m(n, rs):
        for r in rs:
            d2d(n, r).wait_recv()
            own_m[n, r] = own_m[n, r] + pr_m[n, r]

        def go(rows):
            for r in rs:
                if r < 3:
                    out_m(n, r, rows).start()

        by_core(go)

    def finish_t():
        for r in range(4):
            d2d_t(r).wait_recv()
            own_t[r] = own_t[r] + pr_t[r]
            if r < 3:
                out_t(r).start()

    tail_copy.wait()
    step1(lambda p, q: atail[p, q], 0)
    pl.semaphore_wait(barrier, 4)
    for r in range(4):
        w = step2(64, lt_mat[:, 0:64], r)
        for c in range(3):
            own_t[r, 16 * c:16 * c + 16, :] = w[0:16, 128 * c:128 * c + 128]
            ps_t[r, 16 * c:16 * c + 16, :] = w[16:32, 128 * c:128 * c + 128]
        d2d_t(r).start()
    for qp in range(4):
        a_copy(1, qp, 1).start()

    def body(n, carry):
        slot = lax.rem(n, 2)
        for qp in range(4):
            a_copy(n, qp, slot).wait()
            step1(lambda p, q: abuf[slot, qp, p, q], qp)

            @pl.when(n + 2 < NM)
            def _():
                a_copy(n + 2, qp, slot).start()

            if qp == 1:
                @pl.when(n == 0)
                def _():
                    finish_t()

                @pl.when(n > 0)
                def _():
                    finish_m(n - 1, (2, 3))

        for r in range(4):
            w = step2(256, l_mat[...], r)
            pack(own_m.at[n, r], w[0:64])
            pack(ps_m.at[n, r], w[64:128])
            d2d(n, r).start()
        finish_m(n, (0, 1))
        return carry

    lax.fori_loop(0, NM, body, 0)
    finish_m(NM - 1, (2, 3))

    def arrive(n, carry):
        def wait(rows):
            for r in range(3):
                out_m(n, r, rows).wait_recv()

        by_core(wait)
        return carry

    lane8 = iota((8, 128), 1)

    def w_rows(i, ns):
        def block(n, b):
            near = own_m[n, 3, b:b + 8, :] + rb_m[1, n, b:b + 8, :]
            far = rb_m[2, n, b:b + 8, :] + rb_m[0, n, b:b + 8, :]
            return near, far

        near, far = [], []
        for n in ns:
            b = 24 * i - 8 if i else 0
            cols = [block(n, b), block(n, b + 8)]
            if i:
                s = block(n, b + 16)
            else:
                s = [jnp.zeros((8, 128), F32)] * 2
                for m in range(5):
                    piece = block(n, 24 * (m + 1) + 8)
                    here = (lane8 >= 24 * m) & (lane8 < min(104, 24 * m + 24))
                    s = [jnp.where(here, pltpu.roll(v, 24 * m + 24, 1), o) for v, o in zip(piece, s)]
            cols.append(s)
            near.append(jnp.concatenate([c[0] for c in cols], axis=1))
            far.append(jnp.concatenate([c[1] for c in cols], axis=1))
        return near + far

    for r in range(3):
        out_t(r).wait_recv()
    lax.fori_loop(0, N1, arrive, 0)
    tails = [jnp.concatenate([own_t[3, 16 * c:16 * c + 16, :] + rb_t[1, 16 * c:16 * c + 16, :] for c in range(3)], axis=1),
             jnp.concatenate([rb_t[2, 16 * c:16 * c + 16, :] + rb_t[0, 16 * c:16 * c + 16, :] for c in range(3)], axis=1)]
    kg = fold(iota((NV, 3 * K1), 1), K1)
    which = jnp.where(kg < 2 * h1, -1, ((kg - 2 * h1) & 15) >> 1)
    for i in range(8):
        w = jnp.concatenate(w_rows(i, range(N1)) + tails, axis=0)
        lhs = jnp.where((which < 0) | (which == i), g1_mat[...], 0.0).astype(BF16)
        v_acc[i] = dot(lhs, parts(w))

    lax.fori_loop(N1, NM, arrive, 0)

    def home(i):
        return pltpu.make_async_copy(v_own.at[i], out_hbm.at[core * 8 + i], o_sem.at[i])

    def back(i):
        return pltpu.make_async_remote_copy(
            src_ref=v_other.at[i], dst_ref=out_hbm.at[core * 8 + i], send_sem=v_send.at[i], recv_sem=v_recv.at[i],
            device_id=partner, device_id_type=MESH)

    def back_in(i):
        return pltpu.make_async_remote_copy(
            src_ref=v_other.at[i], dst_ref=out_hbm.at[(1 - core) * 8 + i], send_sem=v_send.at[i], recv_sem=v_recv.at[i],
            device_id=partner, device_id_type=MESH)

    for i in range(8):
        w = jnp.concatenate(w_rows(i, range(N1, NM)), axis=0)
        v = v_acc[i] + dot(g2_mat[...], parts(w))
        c0, c1, c2 = v[:, 0:128], v[:, 128:256], v[:, 256:384]
        c3 = pltpu.roll(c2, 76, 1)
        mine_v = jnp.concatenate([jnp.where(core == 0, c0, c1), jnp.where(core == 0, c2, c3)], axis=1)
        theirs = jnp.concatenate([jnp.where(core == 0, c1, c0), jnp.where(core == 0, c3, c2)], axis=1)
        v_own[i] = mine_v[:, 0:180]
        v_other[i] = theirs[:, 0:180]
        if i < 7:
            back(i).start()
            home(i).start()
        else:
            @pl.when(core == 0)
            def _():
                back(7).start()
                home(7).start()

    for i in range(7):
        home(i).wait()
        back(i).wait_send()
        back_in(i).wait_recv()

    @pl.when(core == 0)
    def _():
        home(7).wait()
        back(7).wait_send()

    @pl.when(core == 1)
    def _():
        back_in(7).wait_recv()

    for r in range(4):
        d2d_t(r).wait_send()
    for r in range(3):
        out_t(r).wait_send()

    def drain(n, carry):
        for r in range(4):
            d2d(n, r).wait_send()

        def wait(rows):
            for r in range(3):
                out_m(n, r, rows).wait_send()

        by_core(wait)
        return carry

    lax.fori_loop(0, NM, drain, 0)


def solution(mesh):
    def local_program(ints_blk, c_occ, c_vir):
        return pl.pallas_call(
            kernel,
            out_shape=jax.ShapeDtypeStruct((NO, NV, 180), F32),
            in_specs=[pl.BlockSpec(memory_space=pl.ANY)] * 3,
            out_specs=pl.BlockSpec(memory_space=pl.ANY),
            scratch_shapes=[
                pltpu.VMEM((2, 4, NP, 2, NB, NB), BF16),
                pltpu.VMEM((NP, QT, NB, NB), BF16),
                pltpu.VMEM((NO, NB), BF16),
                pltpu.VMEM((NV, NB), BF16),
                pltpu.VMEM((16, 128), F32),
                pltpu.VMEM((128, 128), F32),
                pltpu.VMEM((128, 1024), BF16),
                pltpu.VMEM((4, 128 * NJ, LW), BF16),
                pltpu.VMEM((128, 256), BF16),
                pltpu.VMEM((32, 256), BF16),
                pltpu.VMEM((NV, 3 * K1), F32),
                pltpu.VMEM((NV, 3 * K2), BF16),
                pltpu.VMEM((NO, 256, 128), BF16),
                pltpu.VMEM((NM, 4, RW, 128), F32),
                pltpu.VMEM((4, 48, 128), F32),
                pltpu.VMEM((NM, 4, RW, 128), F32),
                pltpu.VMEM((4, 48, 128), F32),
                pltpu.VMEM((NM, 4, RW, 128), F32),
                pltpu.VMEM((4, 48, 128), F32),
                pltpu.VMEM((3, NM, RW, 128), F32),
                pltpu.VMEM((3, 48, 128), F32),
                pltpu.VMEM((8, NV, LW), F32),
                pltpu.VMEM((8, NV, 180), F32),
                pltpu.VMEM((8, NV, 180), F32),
                pltpu.SemaphoreType.DMA((2, 4)),
                pltpu.SemaphoreType.DMA,
                pltpu.SemaphoreType.DMA((2,)),
                pltpu.SemaphoreType.DMA((NM + 1, 4)),
                pltpu.SemaphoreType.DMA((NM + 1, 4)),
                pltpu.SemaphoreType.DMA((NM + 1, 3)),
                pltpu.SemaphoreType.DMA((NM + 1, 3)),
                pltpu.SemaphoreType.DMA((8,)),
                pltpu.SemaphoreType.DMA((8,)),
                pltpu.SemaphoreType.DMA((8,)),
            ],
            compiler_params=pltpu.CompilerParams(
                collective_id=0, has_side_effects=True, vmem_limit_bytes=60 * 1024 * 1024),
            name='four_index',
        )(ints_blk, c_occ.T, c_vir.T)

    return jax.shard_map(
        local_program,
        mesh=mesh,
        in_specs=(P(('frag', 'dev'), 'dev2', None, None), P('frag', None), P('frag', None)),
        out_specs=P(None, None, ('frag', 'dev2', 'dev')),
        check_vma=False,
    )
```

time: 296 us -> 48.4 us (0.16); the launches traced: 291 us -> 48.3 us
  blocking collectives: 134 us -> 0 us
  local copies, waits for them, and re-layouts: 114 us -> 2.98 us
  Pallas kernels: 0 us -> 45.3 us
  matrix products: 41.3 us -> 0 us
    all_to_all x2 -> x0, blocking collectives: 134 us -> none  [the longest x1 70.3 us: local_program(): half_ints = lax.all_to_all(half_ints, 'dev', 2, 0, tiled=True)]
    unnamed x6 -> x0, local copies, waits for them, and re-layouts: 55.4 us -> none
    pallas_call x0 -> x1, Pallas kernels: none -> 45.3 us  [local_program(): pl.pallas_call(kernel, out_shape=jax.ShapeDtypeStruct((NO, NV, 180), F32)...]
    dot_general x4 -> x0, matrix products: 41.3 us -> none  [the longest x1 21.5 us: local_program(): jnp.einsum('pqrs,rj->pqsj', ints_blk, c_occ, preferred_element_type=jnp.f...]
    all_to_all x4 -> x0, local copies, waits for them, and re-layouts: 37.5 us -> none  [the longest x3 35.4 us: local_program(): half_ints = lax.all_to_all(half_ints, 'dev2', 2, 1, tiled=True)]
    reshape x1 -> x0, local copies, waits for them, and re-layouts: 20 us -> none  [local_program(): half_ints = half_ints.reshape(rows_p, rows_q, n_occ * n_virt)]
    pallas_call x0 -> x1, local copies, waits for them, and re-layouts: none -> 2.98 us  [local_program(): pl.pallas_call(kernel, out_shape=jax.ShapeDtypeStruct((NO, NV, 180), F32)...]
where the time goes in v2:
time: 48.4 us; the launch traced here: 48.3 us
  Pallas kernels  45.3 us (94%)
  local copies, waits for them, and re-layouts  2.98 us (6%)
    pallas_call x1, Pallas kernels, local_program(): pl.pallas_call(kernel, out_shape=jax.ShapeDtypeStruct((NO, NV, 180), F32)...  45.3 us
    pallas_call x1, local copies, waits for them, and re-layouts, local_program(): pl.pallas_call(kernel, out_shape=jax.ShapeDtypeStruct((NO, NV, 180), F32)...  2.98 us

profile of v2, /device:TPU:0, one launch (start us, length us, event | category | flops | bytes accessed | tf_op | source)
XLA Modules:
  0.0 48.3 jit_solution(6311113020614124990)
XLA Ops:
  0.0 45.3 %four_index.1 = f32[15,96,180]{2,1,0:T(8,128)} custom-call(bf16[29,58,116,116]{3,2,1,0:T(8,128)(2,1)} %a_hbm.1, bf16[15,116]{1,0:T(8,128)(2,1)} %bitcast.3, bf16[96,116]{1,0:T(8,128)(2,1)} %bitcast.2), custom_call_target="tpu_custom_call" | custom-call | tf_op jit(solution)/shard_map/four_index/pallas_call | solution.py:356
  45.3 3.0 %copy.4 = f32[15,96,180]{1,2,0:T(8,128)} copy(f32[15,96,180]{2,1,0:T(8,128)} %four_index.1) | data formatting | bytes 2073600 | tf_op jit(solution)/shard_map/four_index/pallas_call | solution.py:356

commit v3 on v2

v3 whole, which is shorter than its diff:
```python
import jax
import jax.numpy as jnp
from jax import lax
from jax.experimental import pallas as pl
from jax.experimental.pallas import tpu as pltpu
from jax.sharding import PartitionSpec as P

MESH = pl.DeviceIdType.MESH
F32, BF16, I32 = jnp.float32, jnp.bfloat16, jnp.int32

NP, NQ, NB = 29, 58, 116
NO, NV = 15, 96
QC = 8
NM = NQ // QC
QT = NQ - NM * QC
PG = 4
L = 128
LW = 3 * L
SP = 108
PW, NS = L - SP, 6
NC, CH = 180, 184
RW = 184
ROWS = (RW, RW - 24)
N1 = NM - 1


def place_of(i, c):
    return 3 * i - 1 + c if i else c


def cols(k, n=1):
    return slice(L * k, L * (k + n))


def rows8(k, n=1):
    return slice(8 * k, 8 * (k + n))


def iota(shape, dim):
    return lax.broadcasted_iota(I32, shape, dim)


def dot(a, b):
    return jnp.dot(a, b, preferred_element_type=F32)


def parts(w):
    hi = w.astype(BF16)
    rest = w - hi.astype(F32)
    mid = rest.astype(BF16)
    lo = (rest - mid.astype(F32)).astype(BF16)
    return jnp.concatenate([hi, mid, lo], axis=1)


def kernel(a_hbm, cot_hbm, cvt_hbm, out_hbm, abuf, atail, cot_in, cvt_in, cot, cvt, s_mat, b_mat, bs_mat, l_mat, lt_mat,
           f1_mat, f2_mat, x_buf, own_m, own_t, ps_m, ps_t, pr_m, pr_t, rb_m, rb_t, v_acc, v_fin,
           a_sem, at_sem, c_sem, d_send, d_recv, r_send, r_recv, v_send, v_recv, o_sem):
    y = lax.axis_index('dev2')
    dev = lax.axis_index('dev')
    core = lax.rem(dev, 2)
    x = dev // 2
    partner = (0, y, x * 2 + (1 - core))
    peers = [(0, 1 - y, (1 - x) * 2 + core), (0, y, (1 - x) * 2 + core), (0, 1 - y, x * 2 + core)]
    chip = [2 * (1 - y) + (1 - x), 2 * y + (1 - x), 2 * (1 - y) + x, 2 * y + x]

    def a_copy(n, qp, slot):
        return pltpu.make_async_copy(
            a_hbm.at[:, pl.ds(n * QC + 2 * qp, 2)], abuf.at[slot, qp], a_sem.at[slot, qp])

    small = [pltpu.make_async_copy(cot_hbm, cot_in, c_sem.at[0]), pltpu.make_async_copy(cvt_hbm, cvt_in, c_sem.at[1])]
    tail_copy = pltpu.make_async_copy(a_hbm.at[:, pl.ds(NM * QC, QT)], atail, at_sem)
    for c in small:
        c.start()
    tail_copy.start()

    barrier = pltpu.get_barrier_semaphore()
    for other in [partner] + peers:
        pl.semaphore_signal(barrier, inc=1, device_id=other, device_id_type=MESH)

    cot[...] = jnp.zeros_like(cot)
    cvt[...] = jnp.zeros_like(cvt)
    for c in small:
        c.wait()
    cot[0:NO, 0:NB] = cot_in[...].astype(F32)
    cvt[0:NV, 0:NB] = cvt_in[...].astype(F32)
    for qp in range(4):
        a_copy(0, qp, 0).start()
    sub = iota((8, L), 0)
    zero = jnp.zeros((8, L), F32)
    for jj in range(8):
        for p in range(8):
            two = [jnp.where(sub == p, cot[j:j + 1, :], zero) for j in (2 * jj, 2 * jj + 1)]
            s_mat[rows8(2 * jj, 2), cols(p)] = jnp.concatenate(two, axis=0).astype(BF16)
    cv = cvt[...].T.astype(BF16)
    first = [(15 * c) // 4 for c in chip]
    first_s = [4 * c + 2 - c // 3 for c in chip]
    lane, row = iota((L, 256), 1), iota((L, 256), 0)
    want = jnp.where(lane < NC, lane, jnp.where(lane < CH, -100000, lane - 4)) - row
    lane_s, row_s = iota((L, L), 1), iota((L, L), 0)
    want_s = jnp.where(lane_s < SP, lane_s + 252, -100000) - row_s
    bs_mat[...] = jnp.zeros_like(bs_mat)
    for r in range(4):
        for j in range(4):
            place = jnp.where(want == 96 * (first[r] + j) - 360 * chip[r], 1.0, 0.0).astype(BF16)
            b_mat[r, cols(j), :] = dot(cv, place).astype(BF16)
        for j in range(2):
            place = jnp.where(want_s == 96 * (first_s[r] + j) - 360 * chip[r], 1.0, 0.0).astype(BF16)
            h = r % 2
            bs_mat[r // 2, cols(2 * h + j), cols(h)] = dot(cv, place).astype(BF16)
    low, high = cot[0:8, :], cot[8:16, :]
    mine = jnp.concatenate([jnp.where(core == 0, low, high), jnp.where(core == 0, high, low)], axis=0)
    kk = iota((L, 256), 1)
    ploc = ((kk >> 4) & 3) * 8 + (kk & 7)
    pick = (iota((L, 256), 0) == ploc + NP * dev) & (ploc < NP)
    l0 = dot(mine.astype(BF16), jnp.where(pick, 1.0, 0.0).astype(BF16)).astype(BF16)
    row, k2 = iota((L, 256), 0), iota((L, 256), 1)
    e8 = jnp.where((iota((L, 16), 0) >> 3) == iota((L, 16), 1), 1.0, 0.0).astype(BF16)
    l_mat[...] = jnp.where((k2 >> 6) * 2 + ((k2 >> 3) & 1) == (row & 7), dot(e8, l0), 0.0).astype(BF16)
    e2 = jnp.where((iota((32, 16), 0) >> 1) == iota((32, 16), 1), 1.0, 0.0).astype(BF16)
    rowt, kt = iota((32, 256), 0), iota((32, 256), 1)
    lt_mat[...] = jnp.where(((kt >> 3) & 1) == (rowt & 1), dot(e2, l0), 0.0).astype(BF16)

    base, other_base = NQ * y, NQ * (1 - y)

    def f_of(want_q):
        sel = jnp.where(iota((L, L), 1) == want_q, 1.0, 0.0).astype(BF16)
        return dot(sel, cv)

    kf = iota((L, L), 0)
    h1 = QC * N1
    f1_mat[...] = f_of(jnp.where(kf < h1, base + kf, jnp.where(kf < 2 * h1, other_base + kf - h1,
                       jnp.where(kf < 2 * h1 + 16, base, other_base) + NM * QC + (kf & 1))))
    f2 = f_of(jnp.where((kf & 8) == 0, base, other_base) + h1 + (kf & 7))
    for i in range(8):
        mine_f = jnp.where((kf >> 4) == i, f2, 0.0).astype(BF16)
        for k in range(3):
            f2_mat[cols(k), cols(i)] = mine_f

    def step1(tile_of, qp):
        zl = jnp.zeros((NB, L - NB), BF16)
        zs = jnp.zeros((L - NB, L), BF16)

        def tile(p, q):
            t = jnp.concatenate([tile_of(p, q), zl], axis=1)
            return jnp.concatenate([t, zs], axis=0)

        for pg in range(PG):
            ps = range(8 * pg, min(NP, 8 * pg + 8))
            rhs = jnp.concatenate([jnp.concatenate([tile(p, 0), tile(p, 1)], axis=1) for p in ps], axis=0)
            t = dot(s_mat[rows8(0, NO), cols(0, len(ps))], rhs)
            r = rows8(8 * qp + 2 * pg, 2)
            for j in range(NO):
                two = jnp.concatenate([t[rows8(j), cols(k)] for k in range(2)], axis=0)
                x_buf[j, r, :] = two.astype(BF16)

    def step2(rows, lhs, pair):
        def w_of(js, weights):
            t = jnp.concatenate([x_buf[j, 0:rows, :] for j in js], axis=1)
            return dot(lhs, dot(t, weights).astype(BF16))

        w = [w_of([first[r] + j for j in range(4)], b_mat[r]) for r in pair]
        third = w_of([first_s[r] + j for r in pair for j in range(2)], bs_mat[pair[0] // 2])
        return [jnp.concatenate([w[k], third[:, cols(k)]], axis=1) for k in range(2)]

    lane8 = iota((8, L), 1)
    spare = lane8 >= SP

    def pack(ref, w):
        col = [[w[rows8(i), cols(c)] for c in range(3)] for i in range(8)]
        for i in range(8):
            for c in range(3 if i else 2):
                v = col[i][c]
                if c == 2 and i <= NS:
                    v = jnp.where(spare, pltpu.roll(col[0][c], SP - PW * (i - 1), 1), v)
                ref[rows8(place_of(i, c)), :] = v

    def d2d(n, r):
        return pltpu.make_async_remote_copy(
            src_ref=ps_m.at[n, r], dst_ref=pr_m.at[n, r], send_sem=d_send.at[n, r], recv_sem=d_recv.at[n, r],
            device_id=partner, device_id_type=MESH)

    def d2d_t(r):
        return pltpu.make_async_remote_copy(
            src_ref=ps_t.at[r], dst_ref=pr_t.at[r], send_sem=d_send.at[NM, r], recv_sem=d_recv.at[NM, r],
            device_id=partner, device_id_type=MESH)

    def out_m(n, r, rows):
        return pltpu.make_async_remote_copy(
            src_ref=own_m.at[n, r, pl.ds(0, rows)], dst_ref=rb_m.at[r, n, pl.ds(0, rows)],
            send_sem=r_send.at[n, r], recv_sem=r_recv.at[n, r], device_id=peers[r], device_id_type=MESH)

    def out_t(r):
        return pltpu.make_async_remote_copy(
            src_ref=own_t.at[r], dst_ref=rb_t.at[r], send_sem=r_send.at[NM, r], recv_sem=r_recv.at[NM, r],
            device_id=peers[r], device_id_type=MESH)

    def by_core(f):
        for k in range(2):
            @pl.when(core == k)
            def _(k=k):
                f(ROWS[k])

    def finish_m(n, rs):
        for r in rs:
            d2d(n, r).wait_recv()
            own_m[n, r] = own_m[n, r] + pr_m[n, r]

        def go(rows):
            for r in rs:
                if r < 3:
                    out_m(n, r, rows).start()

        by_core(go)

    def finish_t():
        for r in range(4):
            d2d_t(r).wait_recv()
            own_t[r] = own_t[r] + pr_t[r]
            if r < 3:
                out_t(r).start()

    tail_copy.wait()
    step1(lambda p, q: atail[p, q], 0)
    pl.semaphore_wait(barrier, 4)
    for pair in ((0, 1), (2, 3)):
        for r, w in zip(pair, step2(64, lt_mat[:, 0:64], pair)):
            for c in range(3):
                own_t[r, rows8(2 * c, 2), :] = w[rows8(0, 2), cols(c)]
                ps_t[r, rows8(2 * c, 2), :] = w[rows8(2, 2), cols(c)]
        for r in pair:
            d2d_t(r).start()
    for qp in range(4):
        a_copy(1, qp, 1).start()

    def body(n, carry):
        slot = lax.rem(n, 2)
        for half in range(2):
            qps = (2 * half, 2 * half + 1)
            for qp in qps:
                a_copy(n, qp, slot).wait()
            for qp in qps:
                step1(lambda p, q: abuf[slot, qp, p, q], qp)

            @pl.when(n + 2 < NM)
            def _():
                for qp in qps:
                    a_copy(n + 2, qp, slot).start()

            if half == 0:
                @pl.when(n == 0)
                def _():
                    finish_t()

            @pl.when(n > 0)
            def _():
                finish_m(n - 1, qps)

        for pair in ((0, 1), (2, 3)):
            for r, w in zip(pair, step2(256, l_mat[...], pair)):
                pack(own_m.at[n, r], w[rows8(0, 8)])
                pack(ps_m.at[n, r], w[rows8(8, 8)])
            for r in pair:
                d2d(n, r).start()
        return carry

    lax.fori_loop(0, NM, body, 0)
    finish_m(NM - 1, (0, 1))
    finish_m(NM - 1, (2, 3))

    def arrive(n, carry):
        def wait(rows):
            for r in range(3):
                out_m(n, r, rows).wait_recv()

        by_core(wait)
        return carry


    def w_rows(i, ns):
        def block(n, b):
            near = own_m[n, 3, rows8(b), :] + rb_m[1, n, rows8(b), :]
            far = rb_m[2, n, rows8(b), :] + rb_m[0, n, rows8(b), :]
            return near, far

        both = []
        for n in ns:
            parts_of = [block(n, place_of(i, c)) for c in range(3 if i else 2)]
            if not i:
                s = [jnp.zeros((8, L), F32)] * 2
                for m in range(NS):
                    piece = block(n, place_of(m + 1, 2))
                    here = (lane8 >= PW * m) & (lane8 < min(SP, PW * m + PW))
                    s = [jnp.where(here, pltpu.roll(v, PW * m + PW, 1), o) for v, o in zip(piece, s)]
                parts_of.append(s)
            both.append([jnp.concatenate(list(c), axis=1) for c in zip(*parts_of)])
        return [b[0] for b in both] + [b[1] for b in both]

    for r in range(3):
        out_t(r).wait_recv()
    lax.fori_loop(0, N1, arrive, 0)
    two = [rows8(2 * c, 2) for c in range(3)]
    tails = [jnp.concatenate([own_t[3, t, :] + rb_t[1, t, :] for t in two], axis=1),
             jnp.concatenate([rb_t[2, t, :] + rb_t[0, t, :] for t in two], axis=1)]
    which = jnp.where(kf < 2 * h1, -1, ((kf - 2 * h1) & 15) >> 1)

    def turned(w):
        return parts(jnp.concatenate([w[:, cols(c)].T for c in range(3)], axis=0))

    for i in range(8):
        w = jnp.concatenate(w_rows(i, range(N1)) + tails, axis=0)
        f1 = jnp.where((which < 0) | (which == i), f1_mat[...], 0.0).astype(BF16)
        v_acc[i] = dot(turned(w), jnp.concatenate([f1] * 3, axis=0))

    lax.fori_loop(N1, NM, arrive, 0)

    def home(i):
        return pltpu.make_async_copy(v_fin.at[i, core], out_hbm.at[core * 8 + i], o_sem.at[i])

    def back(i):
        return pltpu.make_async_remote_copy(
            src_ref=v_fin.at[i, 1 - core], dst_ref=out_hbm.at[core * 8 + i], send_sem=v_send.at[i],
            recv_sem=v_recv.at[i], device_id=partner, device_id_type=MESH)

    def back_in(i):
        return pltpu.make_async_remote_copy(
            src_ref=v_fin.at[i, 1 - core], dst_ref=out_hbm.at[(1 - core) * 8 + i], send_sem=v_send.at[i],
            recv_sem=v_recv.at[i], device_id=partner, device_id_type=MESH)

    rows = [v for i in range(7) for v in w_rows(i, range(N1, NM))]
    rows += [jnp.where(core == 0, v, 0.0) for v in w_rows(7, range(N1, NM))]
    w = turned(jnp.concatenate(rows, axis=0))
    for g in range(4):
        v = dot(w, f2_mat[:, cols(2 * g, 2)])
        for i in (2 * g, 2 * g + 1):
            vi = v_acc[i] + v[:, cols(i % 2)]
            for h in range(2):
                v_fin[i, h] = vi[CH * h:CH * h + NC, 0:NV]
        for i in (2 * g, 2 * g + 1):
            if i < 7:
                back(i).start()
                home(i).start()
            else:
                @pl.when(core == 0)
                def _():
                    back(7).start()
                    home(7).start()

    for i in range(7):
        home(i).wait()
        back(i).wait_send()
        back_in(i).wait_recv()

    @pl.when(core == 0)
    def _():
        home(7).wait()
        back(7).wait_send()

    @pl.when(core == 1)
    def _():
        back_in(7).wait_recv()

    for r in range(4):
        d2d_t(r).wait_send()
    for r in range(3):
        out_t(r).wait_send()

    def drain(n, carry):
        for r in range(4):
            d2d(n, r).wait_send()

        def wait(rows):
            for r in range(3):
                out_m(n, r, rows).wait_send()

        by_core(wait)
        return carry

    lax.fori_loop(0, NM, drain, 0)


def solution(mesh):
    def local_program(ints_blk, c_occ, c_vir):
        v = pl.pallas_call(
            kernel,
            out_shape=jax.ShapeDtypeStruct((NO, NC, NV), F32),
            in_specs=[pl.BlockSpec(memory_space=pl.ANY)] * 3,
            out_specs=pl.BlockSpec(memory_space=pl.ANY),
            scratch_shapes=[
                pltpu.VMEM((2, 4, NP, 2, NB, NB), BF16),
                pltpu.VMEM((NP, QT, NB, NB), BF16),
                pltpu.VMEM((NO, NB), BF16),
                pltpu.VMEM((NV, NB), BF16),
                pltpu.VMEM((16, L), F32),
                pltpu.VMEM((L, L), F32),
                pltpu.VMEM((L, 1024), BF16),
                pltpu.VMEM((4, 512, 256), BF16),
                pltpu.VMEM((2, 512, 256), BF16),
                pltpu.VMEM((L, 256), BF16),
                pltpu.VMEM((32, 256), BF16),
                pltpu.VMEM((L, L), F32),
                pltpu.VMEM((384, 1024), BF16),
                pltpu.VMEM((NO, 256, L), BF16),
                pltpu.VMEM((NM, 4, RW, L), F32),
                pltpu.VMEM((4, 48, L), F32),
                pltpu.VMEM((NM, 4, RW, L), F32),
                pltpu.VMEM((4, 48, L), F32),
                pltpu.VMEM((NM, 4, RW, L), F32),
                pltpu.VMEM((4, 48, L), F32),
                pltpu.VMEM((3, NM, RW, L), F32),
                pltpu.VMEM((3, 48, L), F32),
                pltpu.VMEM((8, LW, L), F32),
                pltpu.VMEM((8, 2, NC, NV), F32),
                pltpu.SemaphoreType.DMA((2, 4)),
                pltpu.SemaphoreType.DMA,
                pltpu.SemaphoreType.DMA((2,)),
                pltpu.SemaphoreType.DMA((NM + 1, 4)),
                pltpu.SemaphoreType.DMA((NM + 1, 4)),
                pltpu.SemaphoreType.DMA((NM + 1, 3)),
                pltpu.SemaphoreType.DMA((NM + 1, 3)),
                pltpu.SemaphoreType.DMA((8,)),
                pltpu.SemaphoreType.DMA((8,)),
                pltpu.SemaphoreType.DMA((8,)),
            ],
            compiler_params=pltpu.CompilerParams(
                collective_id=0, has_side_effects=True, vmem_limit_bytes=60 * 1024 * 1024),
            name='four_index',
        )(ints_blk, c_occ.T, c_vir.T)
        return v.transpose(0, 2, 1)

    return jax.shard_map(
        local_program,
        mesh=mesh,
        in_specs=(P(('frag', 'dev'), 'dev2', None, None), P('frag', None), P('frag', None)),
        out_specs=P(None, None, ('frag', 'dev2', 'dev')),
        check_vma=False,
    )
```

time: 48.4 us -> 46 us (0.950)
  Pallas kernels: 45.3 us -> 43.4 us
    pallas_call x1 -> x0, local copies, waits for them, and re-layouts: 2.98 us -> none  [local_program(): pl.pallas_call(kernel, out_shape=jax.ShapeDtypeStruct((NO, NV, 180), F32)...]
    unnamed x0 -> x1, local copies, waits for them, and re-layouts: none -> 2.53 us
    pallas_call x1, Pallas kernels: 45.3 us -> 43.4 us  [local_program(): pl.pallas_call(kernel, out_shape=jax.ShapeDtypeStruct((NO, NC, NV), F32),...]
where the time goes in v3:
time: 46 us; the launch traced here: 45.9 us
  Pallas kernels  43.4 us (94%)
  local copies, waits for them, and re-layouts  2.53 us (5%)
    pallas_call x1, Pallas kernels, local_program(): pl.pallas_call(kernel, out_shape=jax.ShapeDtypeStruct((NO, NC, NV), F32),...  43.4 us
    unnamed x1, local copies, waits for them, and re-layouts  2.53 us

profile of v3, /device:TPU:0, one launch (start us, length us, event | category | flops | bytes accessed | tf_op | source)
XLA Modules:
  0.0 45.9 jit_solution(15355094409331528319)
XLA Ops:
  0.0 43.4 %four_index.1 = f32[15,180,96]{2,1,0:T(8,128)} custom-call(bf16[29,58,116,116]{3,2,1,0:T(8,128)(2,1)} %a_hbm.1, bf16[15,116]{1,0:T(8,128)(2,1)} %bitcast.5, bf16[96,116]{1,0:T(8,128)(2,1)} %bitcast.4), custom_call_target="tpu_custom_call" | custom-call | tf_op jit(solution)/shard_map/four_index/pallas_call | solution.py:383
  43.4 2.5 %copy.5 = f32[15,96,180]{1,2,0:T(8,128)} copy(f32[15,96,180]{1,2,0:T(8,128)} %bitcast.3) | data formatting | bytes 2073600

commit v4 on v3

--- a/solution.py
+++ b/solution.py
@@ -53,7 +53,7 @@
 
 
 def kernel(a_hbm, cot_hbm, cvt_hbm, out_hbm, abuf, atail, cot_in, cvt_in, cot, cvt, s_mat, b_mat, bs_mat, l_mat, lt_mat,
-           f1_mat, f2_mat, x_buf, own_m, own_t, ps_m, ps_t, pr_m, pr_t, rb_m, rb_t, v_acc, v_fin,
+           f1_mat, f2_mat, x_buf, h_buf, own_m, own_t, ps_m, ps_t, pr_m, pr_t, rb_m, rb_t, v_acc, v_fin,
            a_sem, at_sem, c_sem, d_send, d_recv, r_send, r_recv, v_send, v_recv, o_sem):
     y = lax.axis_index('dev2')
     dev = lax.axis_index('dev')
@@ -153,14 +153,18 @@
                 two = jnp.concatenate([t[rows8(j), cols(k)] for k in range(2)], axis=0)
                 x_buf[j, r, :] = two.astype(BF16)
 
-    def step2(rows, lhs, pair):
-        def w_of(js, weights):
-            t = jnp.concatenate([x_buf[j, 0:rows, :] for j in js], axis=1)
-            return dot(lhs, dot(t, weights).astype(BF16))
-
-        w = [w_of([first[r] + j for j in range(4)], b_mat[r]) for r in pair]
-        third = w_of([first_s[r] + j for r in pair for j in range(2)], bs_mat[pair[0] // 2])
-        return [jnp.concatenate([w[k], third[:, cols(k)]], axis=1) for k in range(2)]
+    def stage_h(rows, k):
+        p, t = k // 3, k % 3
+        if t < 2:
+            js, weights = [first[2 * p + t] + j for j in range(4)], b_mat[2 * p + t]
+        else:
+            js, weights = [first_s[r] + j for r in (2 * p, 2 * p + 1) for j in range(2)], bs_mat[p]
+        lhs = jnp.concatenate([x_buf[j, 0:rows, :] for j in js], axis=1)
+        h_buf[k, 0:rows, :] = dot(lhs, weights).astype(BF16)
+
+    def stage_w(rows, lhs, p):
+        w = [dot(lhs, h_buf[3 * p + t, 0:rows, :]) for t in range(3)]
+        return [jnp.concatenate([w[k], w[2][:, cols(k)]], axis=1) for k in range(2)]
 
     lane8 = iota((8, L), 1)
     spare = lane8 >= SP
@@ -222,8 +226,11 @@
     tail_copy.wait()
     step1(lambda p, q: atail[p, q], 0)
     pl.semaphore_wait(barrier, 4)
-    for pair in ((0, 1), (2, 3)):
-        for r, w in zip(pair, step2(64, lt_mat[:, 0:64], pair)):
+    for k in range(6):
+        stage_h(64, k)
+    for p in range(2):
+        pair = (2 * p, 2 * p + 1)
+        for r, w in zip(pair, stage_w(64, lt_mat[:, 0:64], p)):
             for c in range(3):
                 own_t[r, rows8(2 * c, 2), :] = w[rows8(0, 2), cols(c)]
                 ps_t[r, rows8(2 * c, 2), :] = w[rows8(2, 2), cols(c)]
@@ -255,8 +262,11 @@
             def _():
                 finish_m(n - 1, qps)
 
-        for pair in ((0, 1), (2, 3)):
-            for r, w in zip(pair, step2(256, l_mat[...], pair)):
+        for k in range(6):
+            stage_h(256, k)
+        for p in range(2):
+            pair = (2 * p, 2 * p + 1)
+            for r, w in zip(pair, stage_w(256, l_mat[...], p)):
                 pack(own_m.at[n, r], w[rows8(0, 8)])
                 pack(ps_m.at[n, r], w[rows8(8, 8)])
             for r in pair:
@@ -311,7 +321,24 @@
         f1 = jnp.where((which < 0) | (which == i), f1_mat[...], 0.0).astype(BF16)
         v_acc[i] = dot(turned(w), jnp.concatenate([f1] * 3, axis=0))
 
-    lax.fori_loop(N1, NM, arrive, 0)
+    for r in range(4):
+        d2d_t(r).wait_send()
+    for r in range(3):
+        out_t(r).wait_send()
+
+    def drain(n, carry):
+        for r in range(4):
+            d2d(n, r).wait_send()
+
+        def wait(rows):
+            for r in range(3):
+                out_m(n, r, rows).wait_send()
+
+        by_core(wait)
+        return carry
+
+    lax.fori_loop(0, N1, drain, 0)
+    arrive(N1, 0)
 
     def home(i):
         return pltpu.make_async_copy(v_fin.at[i, core], out_hbm.at[core * 8 + i], o_sem.at[i])
@@ -329,21 +356,22 @@
     rows = [v for i in range(7) for v in w_rows(i, range(N1, NM))]
     rows += [jnp.where(core == 0, v, 0.0) for v in w_rows(7, range(N1, NM))]
     w = turned(jnp.concatenate(rows, axis=0))
-    for g in range(4):
-        v = dot(w, f2_mat[:, cols(2 * g, 2)])
+    vs = [dot(w, f2_mat[:, cols(2 * g, 2)]) for g in range(4)]
+    for g, v in enumerate(vs):
         for i in (2 * g, 2 * g + 1):
             vi = v_acc[i] + v[:, cols(i % 2)]
             for h in range(2):
                 v_fin[i, h] = vi[CH * h:CH * h + NC, 0:NV]
-        for i in (2 * g, 2 * g + 1):
-            if i < 7:
-                back(i).start()
-                home(i).start()
-            else:
-                @pl.when(core == 0)
-                def _():
-                    back(7).start()
-                    home(7).start()
+        if g % 2:
+            for i in range(2 * g - 2, 2 * g + 2):
+                if i < 7:
+                    back(i).start()
+                    home(i).start()
+                else:
+                    @pl.when(core == 0)
+                    def _():
+                        back(7).start()
+                        home(7).start()
 
     for i in range(7):
         home(i).wait()
@@ -358,24 +386,7 @@
     @pl.when(core == 1)
     def _():
         back_in(7).wait_recv()
-
-    for r in range(4):
-        d2d_t(r).wait_send()
-    for r in range(3):
-        out_t(r).wait_send()
-
-    def drain(n, carry):
-        for r in range(4):
-            d2d(n, r).wait_send()
-
-        def wait(rows):
-            for r in range(3):
-                out_m(n, r, rows).wait_send()
-
-        by_core(wait)
-        return carry
-
-    lax.fori_loop(0, NM, drain, 0)
+    drain(NM - 1, 0)
 
 
 def solution(mesh):
@@ -400,6 +411,7 @@
                 pltpu.VMEM((L, L), F32),
                 pltpu.VMEM((384, 1024), BF16),
                 pltpu.VMEM((NO, 256, L), BF16),
+                pltpu.VMEM((6, 256, 256), BF16),
                 pltpu.VMEM((NM, 4, RW, L), F32),
                 pltpu.VMEM((4, 48, L), F32),
                 pltpu.VMEM((NM, 4, RW, L), F32),

time: 46 us -> 44.7 us (0.972)
  Pallas kernels: 43.4 us -> 42 us
    pallas_call x1, Pallas kernels: 43.4 us -> 42 us  [local_program(): pl.pallas_call(kernel, out_shape=jax.ShapeDtypeStruct((NO, NC, NV), F32),...]
where the time goes in v4:
time: 44.7 us; the launch traced here: 44.5 us
  Pallas kernels  42 us (94%)
  local copies, waits for them, and re-layouts  2.53 us (6%)
    pallas_call x1, Pallas kernels, local_program(): pl.pallas_call(kernel, out_shape=jax.ShapeDtypeStruct((NO, NC, NV), F32),...  42 us
    unnamed x1, local copies, waits for them, and re-layouts  2.53 us

profile of v4, /device:TPU:0, one launch (start us, length us, event | category | flops | bytes accessed | tf_op | source)
XLA Modules:
  0.0 44.5 jit_solution(11148668608168185418)
XLA Ops:
  0.0 42.0 %four_index.1 = f32[15,180,96]{2,1,0:T(8,128)} custom-call(bf16[29,58,116,116]{3,2,1,0:T(8,128)(2,1)} %a_hbm.1, bf16[15,116]{1,0:T(8,128)(2,1)} %bitcast.5, bf16[96,116]{1,0:T(8,128)(2,1)} %bitcast.4), custom_call_target="tpu_custom_call" | custom-call | tf_op jit(solution)/shard_map/four_index/pallas_call | solution.py:394
  42.0 2.5 %copy.5 = f32[15,96,180]{1,2,0:T(8,128)} copy(f32[15,96,180]{1,2,0:T(8,128)} %bitcast.3) | data formatting | bytes 2073600

commit v5 on v4

--- a/solution.py
+++ b/solution.py
@@ -11,8 +11,8 @@
 NP, NQ, NB = 29, 58, 116
 NO, NV = 15, 96
 QC = 8
-NM = NQ // QC
-QT = NQ - NM * QC
+NM = 6
+SMALL = ((48, 2), (50, 4), (54, 4))
 PG = 4
 L = 128
 LW = 3 * L
@@ -52,9 +52,9 @@
     return jnp.concatenate([hi, mid, lo], axis=1)
 
 
-def kernel(a_hbm, cot_hbm, cvt_hbm, out_hbm, abuf, atail, cot_in, cvt_in, cot, cvt, s_mat, b_mat, bs_mat, l_mat, lt_mat,
-           f1_mat, f2_mat, x_buf, h_buf, own_m, own_t, ps_m, ps_t, pr_m, pr_t, rb_m, rb_t, v_acc, v_fin,
-           a_sem, at_sem, c_sem, d_send, d_recv, r_send, r_recv, v_send, v_recv, o_sem):
+def kernel(a_hbm, cot_hbm, cvt_hbm, out_hbm, abuf, as0, as1, as2, cot_in, cvt_in, cot, cvt, s_mat, b_mat, bs_mat, l8, l4, l2,
+           f1_mat, f2_mat, x_buf, h_buf, own_m, own_s, ps_m, ps_s, pr_m, pr_s, rb_m, rb_s, v_acc, v_fin,
+           a_sem, as_sem, c_sem, d_send, d_recv, r_send, r_recv, v_send, v_recv, o_sem):
     y = lax.axis_index('dev2')
     dev = lax.axis_index('dev')
     core = lax.rem(dev, 2)
@@ -68,10 +68,13 @@
             a_hbm.at[:, pl.ds(n * QC + 2 * qp, 2)], abuf.at[slot, qp], a_sem.at[slot, qp])
 
     small = [pltpu.make_async_copy(cot_hbm, cot_in, c_sem.at[0]), pltpu.make_async_copy(cvt_hbm, cvt_in, c_sem.at[1])]
-    tail_copy = pltpu.make_async_copy(a_hbm.at[:, pl.ds(NM * QC, QT)], atail, at_sem)
+    a_small = (as0, as1, as2)
+    small_copy = [pltpu.make_async_copy(a_hbm.at[:, pl.ds(q, nq)], a_small[m], as_sem.at[m])
+                  for m, (q, nq) in enumerate(SMALL)]
     for c in small:
         c.start()
-    tail_copy.start()
+    small_copy[0].start()
+    small_copy[1].start()
 
     barrier = pltpu.get_barrier_semaphore()
     for other in [partner] + peers:
@@ -83,8 +86,6 @@
         c.wait()
     cot[0:NO, 0:NB] = cot_in[...].astype(F32)
     cvt[0:NV, 0:NB] = cvt_in[...].astype(F32)
-    for qp in range(4):
-        a_copy(0, qp, 0).start()
     sub = iota((8, L), 0)
     zero = jnp.zeros((8, L), F32)
     for jj in range(8):
@@ -113,12 +114,13 @@
     ploc = ((kk >> 4) & 3) * 8 + (kk & 7)
     pick = (iota((L, 256), 0) == ploc + NP * dev) & (ploc < NP)
     l0 = dot(mine.astype(BF16), jnp.where(pick, 1.0, 0.0).astype(BF16)).astype(BF16)
-    row, k2 = iota((L, 256), 0), iota((L, 256), 1)
-    e8 = jnp.where((iota((L, 16), 0) >> 3) == iota((L, 16), 1), 1.0, 0.0).astype(BF16)
-    l_mat[...] = jnp.where((k2 >> 6) * 2 + ((k2 >> 3) & 1) == (row & 7), dot(e8, l0), 0.0).astype(BF16)
-    e2 = jnp.where((iota((32, 16), 0) >> 1) == iota((32, 16), 1), 1.0, 0.0).astype(BF16)
-    rowt, kt = iota((32, 256), 0), iota((32, 256), 1)
-    lt_mat[...] = jnp.where(((kt >> 3) & 1) == (rowt & 1), dot(e2, l0), 0.0).astype(BF16)
+    for l_mat, sh in ((l8, 3), (l4, 2), (l2, 1)):
+        nq = 1 << sh
+        rows = 16 * nq
+        e = jnp.where((iota((rows, 16), 0) >> sh) == iota((rows, 16), 1), 1.0, 0.0).astype(BF16)
+        row, k2 = iota((rows, 256), 0), iota((rows, 256), 1)
+        here = (k2 >> 6) * 2 + ((k2 >> 3) & 1) == (row & (nq - 1))
+        l_mat[...] = jnp.where(here, dot(e, l0), 0.0).astype(BF16)
 
     base, other_base = NQ * y, NQ * (1 - y)
 
@@ -128,8 +130,11 @@
 
     kf = iota((L, L), 0)
     h1 = QC * N1
-    f1_mat[...] = f_of(jnp.where(kf < h1, base + kf, jnp.where(kf < 2 * h1, other_base + kf - h1,
-                       jnp.where(kf < 2 * h1 + 16, base, other_base) + NM * QC + (kf & 1))))
+    kt = kf - 2 * h1
+    ks, ku = kt >> 4, kt & 7
+    kq = jnp.where(ks == 0, SMALL[0][0] + (ku & 1), jnp.where(ks == 1, SMALL[1][0], SMALL[2][0]) + (ku & 3))
+    f1_mat[...] = f_of(jnp.where(kt < 0, jnp.where(kf < h1, base + kf, other_base + kf - h1),
+                       jnp.where((kt & 8) == 0, base, other_base) + kq))
     f2 = f_of(jnp.where((kf & 8) == 0, base, other_base) + h1 + (kf & 7))
     for i in range(8):
         mine_f = jnp.where((kf >> 4) == i, f2, 0.0).astype(BF16)
@@ -183,20 +188,22 @@
             src_ref=ps_m.at[n, r], dst_ref=pr_m.at[n, r], send_sem=d_send.at[n, r], recv_sem=d_recv.at[n, r],
             device_id=partner, device_id_type=MESH)
 
-    def d2d_t(r):
-        return pltpu.make_async_remote_copy(
-            src_ref=ps_t.at[r], dst_ref=pr_t.at[r], send_sem=d_send.at[NM, r], recv_sem=d_recv.at[NM, r],
-            device_id=partner, device_id_type=MESH)
+    def d2d_s(m, r):
+        part = pl.ds(0, 24 * SMALL[m][1])
+        return pltpu.make_async_remote_copy(
+            src_ref=ps_s.at[m, r, part], dst_ref=pr_s.at[m, r, part], send_sem=d_send.at[NM + m, r],
+            recv_sem=d_recv.at[NM + m, r], device_id=partner, device_id_type=MESH)
 
     def out_m(n, r, rows):
         return pltpu.make_async_remote_copy(
             src_ref=own_m.at[n, r, pl.ds(0, rows)], dst_ref=rb_m.at[r, n, pl.ds(0, rows)],
             send_sem=r_send.at[n, r], recv_sem=r_recv.at[n, r], device_id=peers[r], device_id_type=MESH)
 
-    def out_t(r):
-        return pltpu.make_async_remote_copy(
-            src_ref=own_t.at[r], dst_ref=rb_t.at[r], send_sem=r_send.at[NM, r], recv_sem=r_recv.at[NM, r],
-            device_id=peers[r], device_id_type=MESH)
+    def out_s(m, r):
+        part = pl.ds(0, 24 * SMALL[m][1])
+        return pltpu.make_async_remote_copy(
+            src_ref=own_s.at[m, r, part], dst_ref=rb_s.at[r, m, part], send_sem=r_send.at[NM + m, r],
+            recv_sem=r_recv.at[NM + m, r], device_id=peers[r], device_id_type=MESH)
 
     def by_core(f):
         for k in range(2):
@@ -216,28 +223,38 @@
 
         by_core(go)
 
-    def finish_t():
+    def finish_s(m):
+        part = rows8(0, 3 * SMALL[m][1])
         for r in range(4):
-            d2d_t(r).wait_recv()
-            own_t[r] = own_t[r] + pr_t[r]
+            d2d_s(m, r).wait_recv()
+            own_s[m, r, part, :] = own_s[m, r, part, :] + pr_s[m, r, part, :]
             if r < 3:
-                out_t(r).start()
-
-    tail_copy.wait()
-    step1(lambda p, q: atail[p, q], 0)
-    pl.semaphore_wait(barrier, 4)
-    for k in range(6):
-        stage_h(64, k)
-    for p in range(2):
-        pair = (2 * p, 2 * p + 1)
-        for r, w in zip(pair, stage_w(64, lt_mat[:, 0:64], p)):
-            for c in range(3):
-                own_t[r, rows8(2 * c, 2), :] = w[rows8(0, 2), cols(c)]
-                ps_t[r, rows8(2 * c, 2), :] = w[rows8(2, 2), cols(c)]
-        for r in pair:
-            d2d_t(r).start()
-    for qp in range(4):
-        a_copy(1, qp, 1).start()
+                out_s(m, r).start()
+
+    small_copy[2].start()
+    for m, (l_mat, a_ref) in enumerate(zip((l2, l4, l4), a_small)):
+        nq = SMALL[m][1]
+        small_copy[m].wait()
+        for qp in range(nq // 2):
+            step1(lambda p, q: a_ref[p, 2 * qp + q], qp)
+        if m == 0:
+            pl.semaphore_wait(barrier, 4)
+        rows = 32 * nq
+        for k in range(6):
+            stage_h(rows, k)
+        for p in range(2):
+            pair = (2 * p, 2 * p + 1)
+            for r, w in zip(pair, stage_w(rows, l_mat[:, 0:rows], p)):
+                for c in range(3):
+                    own_s[m, r, rows8(c * nq, nq), :] = w[rows8(0, nq), cols(c)]
+                    ps_s[m, r, rows8(c * nq, nq), :] = w[rows8(nq, nq), cols(c)]
+            for r in pair:
+                d2d_s(m, r).start()
+        if m < 2:
+            for qp in range(4):
+                a_copy(m, qp, m).start()
+        if m > 0:
+            finish_s(m - 1)
 
     def body(n, carry):
         slot = lax.rem(n, 2)
@@ -253,10 +270,10 @@
                 for qp in qps:
                     a_copy(n + 2, qp, slot).start()
 
-            if half == 0:
+            if half == 1:
                 @pl.when(n == 0)
                 def _():
-                    finish_t()
+                    finish_s(2)
 
             @pl.when(n > 0)
             def _():
@@ -266,7 +283,7 @@
             stage_h(256, k)
         for p in range(2):
             pair = (2 * p, 2 * p + 1)
-            for r, w in zip(pair, stage_w(256, l_mat[...], p)):
+            for r, w in zip(pair, stage_w(256, l8[...], p)):
                 pack(own_m.at[n, r], w[rows8(0, 8)])
                 pack(ps_m.at[n, r], w[rows8(8, 8)])
             for r in pair:
@@ -305,26 +322,36 @@
             both.append([jnp.concatenate(list(c), axis=1) for c in zip(*parts_of)])
         return [b[0] for b in both] + [b[1] for b in both]
 
-    for r in range(3):
-        out_t(r).wait_recv()
+    def small_rows(i):
+        out = []
+        for m, (_, nq) in enumerate(SMALL):
+            own, ins = [], []
+            for c in range(3):
+                t = rows8(c * nq + (i * nq) // 8)
+                own.append(own_s[m, 3, t, :] + rb_s[1, m, t, :])
+                ins.append(rb_s[2, m, t, :] + rb_s[0, m, t, :])
+            out += [jnp.concatenate(own, axis=1), jnp.concatenate(ins, axis=1)]
+        return out
+
+    for m in range(3):
+        for r in range(3):
+            out_s(m, r).wait_recv()
     lax.fori_loop(0, N1, arrive, 0)
-    two = [rows8(2 * c, 2) for c in range(3)]
-    tails = [jnp.concatenate([own_t[3, t, :] + rb_t[1, t, :] for t in two], axis=1),
-             jnp.concatenate([rb_t[2, t, :] + rb_t[0, t, :] for t in two], axis=1)]
-    which = jnp.where(kf < 2 * h1, -1, ((kf - 2 * h1) & 15) >> 1)
 
     def turned(w):
         return parts(jnp.concatenate([w[:, cols(c)].T for c in range(3)], axis=0))
 
     for i in range(8):
-        w = jnp.concatenate(w_rows(i, range(N1)) + tails, axis=0)
-        f1 = jnp.where((which < 0) | (which == i), f1_mat[...], 0.0).astype(BF16)
+        w = jnp.concatenate(w_rows(i, range(N1)) + small_rows(i), axis=0)
+        here = (kt < 0) | ((ks == 0) & (ku >> 1 == i % 4)) | ((ks > 0) & (ku >> 2 == i % 2))
+        f1 = jnp.where(here, f1_mat[...], 0.0).astype(BF16)
         v_acc[i] = dot(turned(w), jnp.concatenate([f1] * 3, axis=0))
 
-    for r in range(4):
-        d2d_t(r).wait_send()
-    for r in range(3):
-        out_t(r).wait_send()
+    for m in range(3):
+        for r in range(4):
+            d2d_s(m, r).wait_send()
+        for r in range(3):
+            out_s(m, r).wait_send()
 
     def drain(n, carry):
         for r in range(4):
@@ -398,7 +425,9 @@
             out_specs=pl.BlockSpec(memory_space=pl.ANY),
             scratch_shapes=[
                 pltpu.VMEM((2, 4, NP, 2, NB, NB), BF16),
-                pltpu.VMEM((NP, QT, NB, NB), BF16),
+                pltpu.VMEM((NP, 2, NB, NB), BF16),
+                pltpu.VMEM((NP, 4, NB, NB), BF16),
+                pltpu.VMEM((NP, 4, NB, NB), BF16),
                 pltpu.VMEM((NO, NB), BF16),
                 pltpu.VMEM((NV, NB), BF16),
                 pltpu.VMEM((16, L), F32),
@@ -407,28 +436,29 @@
                 pltpu.VMEM((4, 512, 256), BF16),
                 pltpu.VMEM((2, 512, 256), BF16),
                 pltpu.VMEM((L, 256), BF16),
+                pltpu.VMEM((64, 256), BF16),
                 pltpu.VMEM((32, 256), BF16),
                 pltpu.VMEM((L, L), F32),
                 pltpu.VMEM((384, 1024), BF16),
                 pltpu.VMEM((NO, 256, L), BF16),
                 pltpu.VMEM((6, 256, 256), BF16),
                 pltpu.VMEM((NM, 4, RW, L), F32),
-                pltpu.VMEM((4, 48, L), F32),
+                pltpu.VMEM((3, 4, 96, L), F32),
                 pltpu.VMEM((NM, 4, RW, L), F32),
-                pltpu.VMEM((4, 48, L), F32),
+                pltpu.VMEM((3, 4, 96, L), F32),
                 pltpu.VMEM((NM, 4, RW, L), F32),
-                pltpu.VMEM((4, 48, L), F32),
+                pltpu.VMEM((3, 4, 96, L), F32),
                 pltpu.VMEM((3, NM, RW, L), F32),
-                pltpu.VMEM((3, 48, L), F32),
+                pltpu.VMEM((3, 3, 96, L), F32),
                 pltpu.VMEM((8, LW, L), F32),
                 pltpu.VMEM((8, 2, NC, NV), F32),
                 pltpu.SemaphoreType.DMA((2, 4)),
-                pltpu.SemaphoreType.DMA,
+                pltpu.SemaphoreType.DMA((3,)),
                 pltpu.SemaphoreType.DMA((2,)),
-                pltpu.SemaphoreType.DMA((NM + 1, 4)),
-                pltpu.SemaphoreType.DMA((NM + 1, 4)),
-                pltpu.SemaphoreType.DMA((NM + 1, 3)),
-                pltpu.SemaphoreType.DMA((NM + 1, 3)),
+                pltpu.SemaphoreType.DMA((NM + 3, 4)),
+                pltpu.SemaphoreType.DMA((NM + 3, 4)),
+                pltpu.SemaphoreType.DMA((NM + 3, 3)),
+                pltpu.SemaphoreType.DMA((NM + 3, 3)),
                 pltpu.SemaphoreType.DMA((8,)),
                 pltpu.SemaphoreType.DMA((8,)),
                 pltpu.SemaphoreType.DMA((8,)),

time: 44.7 us -> 43.6 us (0.975)
  Pallas kernels: 42 us -> 40.9 us
    pallas_call x1, Pallas kernels: 42 us -> 40.9 us  [local_program(): pl.pallas_call(kernel, out_shape=jax.ShapeDtypeStruct((NO, NC, NV), F32),...]
where the time goes in v5:
time: 43.6 us; the launch traced here: 43.5 us
  Pallas kernels  40.9 us (94%)
  local copies, waits for them, and re-layouts  2.53 us (6%)
    pallas_call x1, Pallas kernels, local_program(): pl.pallas_call(kernel, out_shape=jax.ShapeDtypeStruct((NO, NC, NV), F32),...  40.9 us
    unnamed x1, local copies, waits for them, and re-layouts  2.53 us

profile of v5, /device:TPU:0, one launch (start us, length us, event | category | flops | bytes accessed | tf_op | source)
XLA Modules:
  0.0 43.5 jit_solution(3840747116737119138)
XLA Ops:
  0.0 40.9 %four_index.1 = f32[15,180,96]{2,1,0:T(8,128)} custom-call(bf16[29,58,116,116]{3,2,1,0:T(8,128)(2,1)} %a_hbm.1, bf16[15,116]{1,0:T(8,128)(2,1)} %bitcast.5, bf16[96,116]{1,0:T(8,128)(2,1)} %bitcast.4), custom_call_target="tpu_custom_call" | custom-call | tf_op jit(solution)/shard_map/four_index/pallas_call | solution.py:421
  40.9 2.5 %copy.5 = f32[15,96,180]{1,2,0:T(8,128)} copy(f32[15,96,180]{1,2,0:T(8,128)} %bitcast.3) | data formatting | bytes 2073600

commit v6 on v5

--- a/solution.py
+++ b/solution.py
@@ -52,9 +52,9 @@
     return jnp.concatenate([hi, mid, lo], axis=1)
 
 
-def kernel(a_hbm, cot_hbm, cvt_hbm, out_hbm, abuf, as0, as1, as2, cot_in, cvt_in, cot, cvt, s_mat, b_mat, bs_mat, l8, l4, l2,
+def kernel(a_hbm, cot_hbm, cvt_hbm, out_ref, abuf, as0, as1, as2, cot_in, cvt_in, cot, cvt, s_mat, b_mat, bs_mat, l8, l4, l2,
            f1_mat, f2_mat, x_buf, h_buf, own_m, own_s, ps_m, ps_s, pr_m, pr_s, rb_m, rb_s, v_acc, v_fin,
-           a_sem, as_sem, c_sem, d_send, d_recv, r_send, r_recv, v_send, v_recv, o_sem):
+           a_sem, as_sem, c_sem, d_send, d_recv, r_send, r_recv, v_send, v_recv):
     y = lax.axis_index('dev2')
     dev = lax.axis_index('dev')
     core = lax.rem(dev, 2)
@@ -114,7 +114,7 @@
     ploc = ((kk >> 4) & 3) * 8 + (kk & 7)
     pick = (iota((L, 256), 0) == ploc + NP * dev) & (ploc < NP)
     l0 = dot(mine.astype(BF16), jnp.where(pick, 1.0, 0.0).astype(BF16)).astype(BF16)
-    for l_mat, sh in ((l8, 3), (l4, 2), (l2, 1)):
+    def build_l(l_mat, sh):
         nq = 1 << sh
         rows = 16 * nq
         e = jnp.where((iota((rows, 16), 0) >> sh) == iota((rows, 16), 1), 1.0, 0.0).astype(BF16)
@@ -122,24 +122,7 @@
         here = (k2 >> 6) * 2 + ((k2 >> 3) & 1) == (row & (nq - 1))
         l_mat[...] = jnp.where(here, dot(e, l0), 0.0).astype(BF16)
 
-    base, other_base = NQ * y, NQ * (1 - y)
-
-    def f_of(want_q):
-        sel = jnp.where(iota((L, L), 1) == want_q, 1.0, 0.0).astype(BF16)
-        return dot(sel, cv)
-
-    kf = iota((L, L), 0)
-    h1 = QC * N1
-    kt = kf - 2 * h1
-    ks, ku = kt >> 4, kt & 7
-    kq = jnp.where(ks == 0, SMALL[0][0] + (ku & 1), jnp.where(ks == 1, SMALL[1][0], SMALL[2][0]) + (ku & 3))
-    f1_mat[...] = f_of(jnp.where(kt < 0, jnp.where(kf < h1, base + kf, other_base + kf - h1),
-                       jnp.where((kt & 8) == 0, base, other_base) + kq))
-    f2 = f_of(jnp.where((kf & 8) == 0, base, other_base) + h1 + (kf & 7))
-    for i in range(8):
-        mine_f = jnp.where((kf >> 4) == i, f2, 0.0).astype(BF16)
-        for k in range(3):
-            f2_mat[cols(k), cols(i)] = mine_f
+    build_l(l2, 1)
 
     def step1(tile_of, qp):
         zl = jnp.zeros((NB, L - NB), BF16)
@@ -239,6 +222,8 @@
             step1(lambda p, q: a_ref[p, 2 * qp + q], qp)
         if m == 0:
             pl.semaphore_wait(barrier, 4)
+        else:
+            finish_s(m - 1)
         rows = 32 * nq
         for k in range(6):
             stage_h(rows, k)
@@ -253,8 +238,9 @@
         if m < 2:
             for qp in range(4):
                 a_copy(m, qp, m).start()
-        if m > 0:
-            finish_s(m - 1)
+        if m == 0:
+            build_l(l4, 2)
+            build_l(l8, 3)
 
     def body(n, carry):
         slot = lax.rem(n, 2)
@@ -270,7 +256,7 @@
                 for qp in qps:
                     a_copy(n + 2, qp, slot).start()
 
-            if half == 1:
+            if half == 0:
                 @pl.when(n == 0)
                 def _():
                     finish_s(2)
@@ -333,6 +319,27 @@
             out += [jnp.concatenate(own, axis=1), jnp.concatenate(ins, axis=1)]
         return out
 
+    base, other_base = NQ * y, NQ * (1 - y)
+
+    late_cv = cvt[...].T.astype(BF16)
+
+    def f_of(want_q):
+        sel = jnp.where(iota((L, L), 1) == want_q, 1.0, 0.0).astype(BF16)
+        return dot(sel, late_cv)
+
+    kf = iota((L, L), 0)
+    h1 = QC * N1
+    kt = kf - 2 * h1
+    ks, ku = kt >> 4, kt & 7
+    kq = jnp.where(ks == 0, SMALL[0][0] + (ku & 1), jnp.where(ks == 1, SMALL[1][0], SMALL[2][0]) + (ku & 3))
+    f1_mat[...] = f_of(jnp.where(kt < 0, jnp.where(kf < h1, base + kf, other_base + kf - h1),
+                       jnp.where((kt & 8) == 0, base, other_base) + kq))
+    f2 = f_of(jnp.where((kf & 8) == 0, base, other_base) + h1 + (kf & 7))
+    for i in range(8):
+        mine_f = jnp.where((kf >> 4) == i, f2, 0.0).astype(BF16)
+        for k in range(3):
+            f2_mat[cols(k), cols(i)] = mine_f
+
     for m in range(3):
         for r in range(3):
             out_s(m, r).wait_recv()
@@ -367,17 +374,14 @@
     lax.fori_loop(0, N1, drain, 0)
     arrive(N1, 0)
 
-    def home(i):
-        return pltpu.make_async_copy(v_fin.at[i, core], out_hbm.at[core * 8 + i], o_sem.at[i])
-
     def back(i):
         return pltpu.make_async_remote_copy(
-            src_ref=v_fin.at[i, 1 - core], dst_ref=out_hbm.at[core * 8 + i], send_sem=v_send.at[i],
+            src_ref=v_fin.at[i], dst_ref=out_ref.at[core * 8 + i], send_sem=v_send.at[i],
             recv_sem=v_recv.at[i], device_id=partner, device_id_type=MESH)
 
     def back_in(i):
         return pltpu.make_async_remote_copy(
-            src_ref=v_fin.at[i, 1 - core], dst_ref=out_hbm.at[(1 - core) * 8 + i], send_sem=v_send.at[i],
+            src_ref=v_fin.at[i], dst_ref=out_ref.at[(1 - core) * 8 + i], send_sem=v_send.at[i],
             recv_sem=v_recv.at[i], device_id=partner, device_id_type=MESH)
 
     rows = [v for i in range(7) for v in w_rows(i, range(N1, NM))]
@@ -387,27 +391,29 @@
     for g, v in enumerate(vs):
         for i in (2 * g, 2 * g + 1):
             vi = v_acc[i] + v[:, cols(i % 2)]
-            for h in range(2):
-                v_fin[i, h] = vi[CH * h:CH * h + NC, 0:NV]
+            low, high = vi[0:NC, 0:NV], vi[CH:CH + NC, 0:NV]
+            v_fin[i] = jnp.where(core == 0, high, low)
+            if i < 7:
+                out_ref[core * 8 + i] = jnp.where(core == 0, low, high)
+            else:
+                @pl.when(core == 0)
+                def _():
+                    out_ref[7] = low
         if g % 2:
             for i in range(2 * g - 2, 2 * g + 2):
                 if i < 7:
                     back(i).start()
-                    home(i).start()
                 else:
                     @pl.when(core == 0)
                     def _():
                         back(7).start()
-                        home(7).start()
 
     for i in range(7):
-        home(i).wait()
         back(i).wait_send()
         back_in(i).wait_recv()
 
     @pl.when(core == 0)
     def _():
-        home(7).wait()
         back(7).wait_send()
 
     @pl.when(core == 1)
@@ -420,9 +426,9 @@
     def local_program(ints_blk, c_occ, c_vir):
         v = pl.pallas_call(
             kernel,
-            out_shape=jax.ShapeDtypeStruct((NO, NC, NV), F32),
+            out_shape=pltpu.VMEM((NO, NC, NV), F32),
             in_specs=[pl.BlockSpec(memory_space=pl.ANY)] * 3,
-            out_specs=pl.BlockSpec(memory_space=pl.ANY),
+            out_specs=pl.BlockSpec(memory_space=pltpu.VMEM),
             scratch_shapes=[
                 pltpu.VMEM((2, 4, NP, 2, NB, NB), BF16),
                 pltpu.VMEM((NP, 2, NB, NB), BF16),
@@ -451,7 +457,7 @@
                 pltpu.VMEM((3, NM, RW, L), F32),
                 pltpu.VMEM((3, 3, 96, L), F32),
                 pltpu.VMEM((8, LW, L), F32),
-                pltpu.VMEM((8, 2, NC, NV), F32),
+                pltpu.VMEM((8, NC, NV), F32),
                 pltpu.SemaphoreType.DMA((2, 4)),
                 pltpu.SemaphoreType.DMA((3,)),
                 pltpu.SemaphoreType.DMA((2,)),
@@ -461,7 +467,6 @@
                 pltpu.SemaphoreType.DMA((NM + 3, 3)),
                 pltpu.SemaphoreType.DMA((8,)),
                 pltpu.SemaphoreType.DMA((8,)),
-                pltpu.SemaphoreType.DMA((8,)),
             ],
             compiler_params=pltpu.CompilerParams(
                 collective_id=0, has_side_effects=True, vmem_limit_bytes=60 * 1024 * 1024),

time: 43.6 us -> 42.4 us (0.972)
  local copies, waits for them, and re-layouts: 2.53 us -> 1.09 us
    unnamed x1, local copies, waits for them, and re-layouts: 2.53 us -> 1.09 us
where the time goes in v6:
time: 42.4 us; the launch traced here: 42.3 us
  Pallas kernels  41.2 us (97%)
  local copies, waits for them, and re-layouts  1.09 us (3%)
    pallas_call x1, Pallas kernels, local_program(): pl.pallas_call(kernel, out_shape=pltpu.VMEM((NO, NC, NV), F32), in_specs=...  41.2 us
    unnamed x1, local copies, waits for them, and re-layouts  1.09 us

profile of v6, /device:TPU:0, one launch (start us, length us, event | category | flops | bytes accessed | tf_op | source)
XLA Modules:
  0.0 42.3 jit_solution(11057751063928026453)
XLA Ops:
  0.0 41.2 %four_index.1 = f32[15,180,96]{2,1,0:T(8,128)S(1)} custom-call(bf16[29,58,116,116]{3,2,1,0:T(8,128)(2,1)} %a_hbm.1, bf16[15,116]{1,0:T(8,128)(2,1)} %bitcast.5, bf16[96,116]{1,0:T(8,128)(2,1)} %bitcast.4), custom_call_target="tpu_custom_call" | custom-call | tf_op jit(solution)/shard_map/four_index/pallas_call | solution.py:427
  41.2 1.1 %copy.5 = f32[15,96,180]{1,2,0:T(8,128)} copy(f32[15,96,180]{1,2,0:T(8,128)S(1)} %bitcast.3) | data formatting | bytes 2073600

commit v7 on v6

--- a/solution.py
+++ b/solution.py
@@ -54,7 +54,7 @@
 
 def kernel(a_hbm, cot_hbm, cvt_hbm, out_ref, abuf, as0, as1, as2, cot_in, cvt_in, cot, cvt, s_mat, b_mat, bs_mat, l8, l4, l2,
            f1_mat, f2_mat, x_buf, h_buf, own_m, own_s, ps_m, ps_s, pr_m, pr_s, rb_m, rb_s, v_acc, v_fin,
-           a_sem, as_sem, c_sem, d_send, d_recv, r_send, r_recv, v_send, v_recv):
+           a_sem, as_sem, c_sem, d_send, d_recv, ds_sem, r_send, r_recv, rs_send, rs_recv, v_sem):
     y = lax.axis_index('dev2')
     dev = lax.axis_index('dev')
     core = lax.rem(dev, 2)
@@ -63,9 +63,13 @@
     peers = [(0, 1 - y, (1 - x) * 2 + core), (0, y, (1 - x) * 2 + core), (0, 1 - y, x * 2 + core)]
     chip = [2 * (1 - y) + (1 - x), 2 * y + (1 - x), 2 * (1 - y) + x, 2 * y + x]
 
-    def a_copy(n, qp, slot):
+    def a_copy(n, half, slot):
         return pltpu.make_async_copy(
-            a_hbm.at[:, pl.ds(n * QC + 2 * qp, 2)], abuf.at[slot, qp], a_sem.at[slot, qp])
+            a_hbm.at[:, pl.ds(n * QC + 4 * half, 4)], abuf.at[slot, half], a_sem.at[slot, half])
+
+    def all_of(ref, sem):
+        return pltpu.make_async_remote_copy(
+            src_ref=ref, dst_ref=ref, send_sem=sem, recv_sem=sem, device_id=partner, device_id_type=MESH)
 
     small = [pltpu.make_async_copy(cot_hbm, cot_in, c_sem.at[0]), pltpu.make_async_copy(cvt_hbm, cvt_in, c_sem.at[1])]
     a_small = (as0, as1, as2)
@@ -168,25 +172,25 @@
 
     def d2d(n, r):
         return pltpu.make_async_remote_copy(
-            src_ref=ps_m.at[n, r], dst_ref=pr_m.at[n, r], send_sem=d_send.at[n, r], recv_sem=d_recv.at[n, r],
+            src_ref=ps_m.at[n, r], dst_ref=pr_m.at[n, r], send_sem=d_send, recv_sem=d_recv.at[n, r // 2],
             device_id=partner, device_id_type=MESH)
 
     def d2d_s(m, r):
         part = pl.ds(0, 24 * SMALL[m][1])
         return pltpu.make_async_remote_copy(
-            src_ref=ps_s.at[m, r, part], dst_ref=pr_s.at[m, r, part], send_sem=d_send.at[NM + m, r],
-            recv_sem=d_recv.at[NM + m, r], device_id=partner, device_id_type=MESH)
+            src_ref=ps_s.at[m, r, part], dst_ref=pr_s.at[m, r, part], send_sem=ds_sem.at[0, m],
+            recv_sem=ds_sem.at[1, m], device_id=partner, device_id_type=MESH)
 
     def out_m(n, r, rows):
         return pltpu.make_async_remote_copy(
             src_ref=own_m.at[n, r, pl.ds(0, rows)], dst_ref=rb_m.at[r, n, pl.ds(0, rows)],
-            send_sem=r_send.at[n, r], recv_sem=r_recv.at[n, r], device_id=peers[r], device_id_type=MESH)
+            send_sem=r_send, recv_sem=r_recv.at[n // N1], device_id=peers[r], device_id_type=MESH)
 
     def out_s(m, r):
         part = pl.ds(0, 24 * SMALL[m][1])
         return pltpu.make_async_remote_copy(
-            src_ref=own_s.at[m, r, part], dst_ref=rb_s.at[r, m, part], send_sem=r_send.at[NM + m, r],
-            recv_sem=r_recv.at[NM + m, r], device_id=peers[r], device_id_type=MESH)
+            src_ref=own_s.at[m, r, part], dst_ref=rb_s.at[r, m, part], send_sem=rs_send.at[m],
+            recv_sem=rs_recv.at[m], device_id=peers[r], device_id_type=MESH)
 
     def by_core(f):
         for k in range(2):
@@ -195,8 +199,8 @@
                 f(ROWS[k])
 
     def finish_m(n, rs):
+        all_of(pr_m.at[n, pl.ds(rs[0], 2)], d_recv.at[n, rs[0] // 2]).wait_recv()
         for r in rs:
-            d2d(n, r).wait_recv()
             own_m[n, r] = own_m[n, r] + pr_m[n, r]
 
         def go(rows):
@@ -208,8 +212,8 @@
 
     def finish_s(m):
         part = rows8(0, 3 * SMALL[m][1])
+        all_of(pr_s.at[m, :, pl.ds(0, 24 * SMALL[m][1])], ds_sem.at[1, m]).wait_recv()
         for r in range(4):
-            d2d_s(m, r).wait_recv()
             own_s[m, r, part, :] = own_s[m, r, part, :] + pr_s[m, r, part, :]
             if r < 3:
                 out_s(m, r).start()
@@ -236,8 +240,8 @@
             for r in pair:
                 d2d_s(m, r).start()
         if m < 2:
-            for qp in range(4):
-                a_copy(m, qp, m).start()
+            for half in range(2):
+                a_copy(m, half, m).start()
         if m == 0:
             build_l(l4, 2)
             build_l(l8, 3)
@@ -246,15 +250,13 @@
         slot = lax.rem(n, 2)
         for half in range(2):
             qps = (2 * half, 2 * half + 1)
+            a_copy(n, half, slot).wait()
             for qp in qps:
-                a_copy(n, qp, slot).wait()
-            for qp in qps:
-                step1(lambda p, q: abuf[slot, qp, p, q], qp)
+                step1(lambda p, q: abuf[slot, half, p, 2 * (qp % 2) + q], qp)
 
             @pl.when(n + 2 < NM)
             def _():
-                for qp in qps:
-                    a_copy(n + 2, qp, slot).start()
+                a_copy(n + 2, half, slot).start()
 
             if half == 0:
                 @pl.when(n == 0)
@@ -279,15 +281,6 @@
     lax.fori_loop(0, NM, body, 0)
     finish_m(NM - 1, (0, 1))
     finish_m(NM - 1, (2, 3))
-
-    def arrive(n, carry):
-        def wait(rows):
-            for r in range(3):
-                out_m(n, r, rows).wait_recv()
-
-        by_core(wait)
-        return carry
-
 
     def w_rows(i, ns):
         def block(n, b):
@@ -340,10 +333,9 @@
         for k in range(3):
             f2_mat[cols(k), cols(i)] = mine_f
 
-    for m in range(3):
-        for r in range(3):
-            out_s(m, r).wait_recv()
-    lax.fori_loop(0, N1, arrive, 0)
+    for m, (_, nq) in enumerate(SMALL):
+        all_of(rb_s.at[:, m, pl.ds(0, 24 * nq)], rs_recv.at[m]).wait_recv()
+    by_core(lambda rows: all_of(rb_m.at[:, pl.ds(0, N1), pl.ds(0, rows)], r_recv.at[0]).wait_recv())
 
     def turned(w):
         return parts(jnp.concatenate([w[:, cols(c)].T for c in range(3)], axis=0))
@@ -354,35 +346,16 @@
         f1 = jnp.where(here, f1_mat[...], 0.0).astype(BF16)
         v_acc[i] = dot(turned(w), jnp.concatenate([f1] * 3, axis=0))
 
-    for m in range(3):
-        for r in range(4):
-            d2d_s(m, r).wait_send()
-        for r in range(3):
-            out_s(m, r).wait_send()
-
-    def drain(n, carry):
-        for r in range(4):
-            d2d(n, r).wait_send()
-
-        def wait(rows):
-            for r in range(3):
-                out_m(n, r, rows).wait_send()
-
-        by_core(wait)
-        return carry
-
-    lax.fori_loop(0, N1, drain, 0)
-    arrive(N1, 0)
+    for m, (_, nq) in enumerate(SMALL):
+        all_of(ps_s.at[m, :, pl.ds(0, 24 * nq)], ds_sem.at[0, m]).wait_send()
+        all_of(own_s.at[m, pl.ds(0, 3), pl.ds(0, 24 * nq)], rs_send.at[m]).wait_send()
+    all_of(ps_m, d_send).wait_send()
+    by_core(lambda rows: all_of(rb_m.at[:, N1, pl.ds(0, rows)], r_recv.at[1]).wait_recv())
 
     def back(i):
         return pltpu.make_async_remote_copy(
-            src_ref=v_fin.at[i], dst_ref=out_ref.at[core * 8 + i], send_sem=v_send.at[i],
-            recv_sem=v_recv.at[i], device_id=partner, device_id_type=MESH)
-
-    def back_in(i):
-        return pltpu.make_async_remote_copy(
-            src_ref=v_fin.at[i], dst_ref=out_ref.at[(1 - core) * 8 + i], send_sem=v_send.at[i],
-            recv_sem=v_recv.at[i], device_id=partner, device_id_type=MESH)
+            src_ref=v_fin.at[i], dst_ref=out_ref.at[core * 8 + i], send_sem=v_sem.at[0], recv_sem=v_sem.at[1],
+            device_id=partner, device_id_type=MESH)
 
     rows = [v for i in range(7) for v in w_rows(i, range(N1, NM))]
     rows += [jnp.where(core == 0, v, 0.0) for v in w_rows(7, range(N1, NM))]
@@ -408,18 +381,13 @@
                     def _():
                         back(7).start()
 
-    for i in range(7):
-        back(i).wait_send()
-        back_in(i).wait_recv()
-
-    @pl.when(core == 0)
-    def _():
-        back(7).wait_send()
-
-    @pl.when(core == 1)
-    def _():
-        back_in(7).wait_recv()
-    drain(NM - 1, 0)
+    def close(rows):
+        n = 8 if rows == RW else 7
+        all_of(own_m.at[:, pl.ds(0, 3), pl.ds(0, rows)], r_send).wait_send()
+        all_of(v_fin.at[pl.ds(0, n)], v_sem.at[0]).wait_send()
+        all_of(out_ref.at[pl.ds(8 if n == 8 else 0, NO - n)], v_sem.at[1]).wait_recv()
+
+    by_core(close)
 
 
 def solution(mesh):
@@ -430,7 +398,7 @@
             in_specs=[pl.BlockSpec(memory_space=pl.ANY)] * 3,
             out_specs=pl.BlockSpec(memory_space=pltpu.VMEM),
             scratch_shapes=[
-                pltpu.VMEM((2, 4, NP, 2, NB, NB), BF16),
+                pltpu.VMEM((2, 2, NP, 4, NB, NB), BF16),
                 pltpu.VMEM((NP, 2, NB, NB), BF16),
                 pltpu.VMEM((NP, 4, NB, NB), BF16),
                 pltpu.VMEM((NP, 4, NB, NB), BF16),
@@ -458,15 +426,17 @@
                 pltpu.VMEM((3, 3, 96, L), F32),
                 pltpu.VMEM((8, LW, L), F32),
                 pltpu.VMEM((8, NC, NV), F32),
-                pltpu.SemaphoreType.DMA((2, 4)),
+                pltpu.SemaphoreType.DMA((2, 2)),
                 pltpu.SemaphoreType.DMA((3,)),
                 pltpu.SemaphoreType.DMA((2,)),
-                pltpu.SemaphoreType.DMA((NM + 3, 4)),
-                pltpu.SemaphoreType.DMA((NM + 3, 4)),
-                pltpu.SemaphoreType.DMA((NM + 3, 3)),
-                pltpu.SemaphoreType.DMA((NM + 3, 3)),
-                pltpu.SemaphoreType.DMA((8,)),
-                pltpu.SemaphoreType.DMA((8,)),
+                pltpu.SemaphoreType.DMA,
+                pltpu.SemaphoreType.DMA((NM, 2)),
+                pltpu.SemaphoreType.DMA((2, 3)),
+                pltpu.SemaphoreType.DMA,
+                pltpu.SemaphoreType.DMA((2,)),
+                pltpu.SemaphoreType.DMA((3,)),
+                pltpu.SemaphoreType.DMA((3,)),
+                pltpu.SemaphoreType.DMA((2,)),
             ],
             compiler_params=pltpu.CompilerParams(
                 collective_id=0, has_side_effects=True, vmem_limit_bytes=60 * 1024 * 1024),

time: 42.4 us -> 41.4 us (0.976)
  Pallas kernels: 41.2 us -> 40.2 us
    pallas_call x1, Pallas kernels: 41.2 us -> 40.2 us  [local_program(): pl.pallas_call(kernel, out_shape=pltpu.VMEM((NO, NC, NV), F32), in_specs=...]
where the time goes in v7:
time: 41.4 us; the launch traced here: 41.3 us
  Pallas kernels  40.2 us (97%)
  local copies, waits for them, and re-layouts  1.09 us (3%)
    pallas_call x1, Pallas kernels, local_program(): pl.pallas_call(kernel, out_shape=pltpu.VMEM((NO, NC, NV), F32), in_specs=...  40.2 us
    unnamed x1, local copies, waits for them, and re-layouts  1.09 us

profile of v7, /device:TPU:0, one launch (start us, length us, event | category | flops | bytes accessed | tf_op | source)
XLA Modules:
  0.0 41.3 jit_solution(7453283495804981612)
XLA Ops:
  0.0 40.2 %four_index.1 = f32[15,180,96]{2,1,0:T(8,128)S(1)} custom-call(bf16[29,58,116,116]{3,2,1,0:T(8,128)(2,1)} %a_hbm.1, bf16[15,116]{1,0:T(8,128)(2,1)} %bitcast.5, bf16[96,116]{1,0:T(8,128)(2,1)} %bitcast.4), custom_call_target="tpu_custom_call" | custom-call | tf_op jit(solution)/shard_map/four_index/pallas_call | solution.py:395
  40.2 1.1 %copy.5 = f32[15,96,180]{1,2,0:T(8,128)} copy(f32[15,96,180]{1,2,0:T(8,128)S(1)} %bitcast.3) | data formatting | bytes 2073600

commit v8 on v7

--- a/solution.py
+++ b/solution.py
@@ -53,8 +53,8 @@
 
 
 def kernel(a_hbm, cot_hbm, cvt_hbm, out_ref, abuf, as0, as1, as2, cot_in, cvt_in, cot, cvt, s_mat, b_mat, bs_mat, l8, l4, l2,
-           f1_mat, f2_mat, x_buf, h_buf, own_m, own_s, ps_m, ps_s, pr_m, pr_s, rb_m, rb_s, v_acc, v_fin,
-           a_sem, as_sem, c_sem, d_send, d_recv, ds_sem, r_send, r_recv, rs_send, rs_recv, v_sem):
+           f1_mat, f2_mat, x_buf, h_buf, own_m, own_s, ps_m, ps_s, pr_m, pr_s, rb_m, rb_s, v_acc, v_in, w2, w2_in,
+           a_sem, as_sem, c_sem, d_send, d_recv, ds_send, ds_recv, r_send, r_recv, rs_send, rs_recv, v_sem, w_sem):
     y = lax.axis_index('dev2')
     dev = lax.axis_index('dev')
     core = lax.rem(dev, 2)
@@ -73,12 +73,12 @@
 
     small = [pltpu.make_async_copy(cot_hbm, cot_in, c_sem.at[0]), pltpu.make_async_copy(cvt_hbm, cvt_in, c_sem.at[1])]
     a_small = (as0, as1, as2)
-    small_copy = [pltpu.make_async_copy(a_hbm.at[:, pl.ds(q, nq)], a_small[m], as_sem.at[m])
+    small_copy = [[pltpu.make_async_copy(a_hbm.at[:, pl.ds(q + 2 * k, 2)], a_small[m].at[:, pl.ds(2 * k, 2)],
+                                         as_sem.at[m, k]) for k in range(nq // 2)]
                   for m, (q, nq) in enumerate(SMALL)]
     for c in small:
         c.start()
-    small_copy[0].start()
-    small_copy[1].start()
+    small_copy[0][0].start()
 
     barrier = pltpu.get_barrier_semaphore()
     for other in [partner] + peers:
@@ -88,6 +88,8 @@
     cvt[...] = jnp.zeros_like(cvt)
     for c in small:
         c.wait()
+    for c in small_copy[1]:
+        c.start()
     cot[0:NO, 0:NB] = cot_in[...].astype(F32)
     cvt[0:NV, 0:NB] = cvt_in[...].astype(F32)
     sub = iota((8, L), 0)
@@ -178,8 +180,8 @@
     def d2d_s(m, r):
         part = pl.ds(0, 24 * SMALL[m][1])
         return pltpu.make_async_remote_copy(
-            src_ref=ps_s.at[m, r, part], dst_ref=pr_s.at[m, r, part], send_sem=ds_sem.at[0, m],
-            recv_sem=ds_sem.at[1, m], device_id=partner, device_id_type=MESH)
+            src_ref=ps_s.at[m, r, part], dst_ref=pr_s.at[m, r, part], send_sem=ds_send.at[m],
+            recv_sem=ds_recv.at[m, r // 2], device_id=partner, device_id_type=MESH)
 
     def out_m(n, r, rows):
         return pltpu.make_async_remote_copy(
@@ -212,17 +214,19 @@
 
     def finish_s(m):
         part = rows8(0, 3 * SMALL[m][1])
-        all_of(pr_s.at[m, :, pl.ds(0, 24 * SMALL[m][1])], ds_sem.at[1, m]).wait_recv()
         for r in range(4):
+            if r % 2 == 0:
+                all_of(pr_s.at[m, pl.ds(r, 2), pl.ds(0, 24 * SMALL[m][1])], ds_recv.at[m, r // 2]).wait_recv()
             own_s[m, r, part, :] = own_s[m, r, part, :] + pr_s[m, r, part, :]
             if r < 3:
                 out_s(m, r).start()
 
-    small_copy[2].start()
+    for c in small_copy[2]:
+        c.start()
     for m, (l_mat, a_ref) in enumerate(zip((l2, l4, l4), a_small)):
         nq = SMALL[m][1]
-        small_copy[m].wait()
         for qp in range(nq // 2):
+            small_copy[m][qp].wait()
             step1(lambda p, q: a_ref[p, 2 * qp + q], qp)
         if m == 0:
             pl.semaphore_wait(barrier, 4)
@@ -338,56 +342,52 @@
     by_core(lambda rows: all_of(rb_m.at[:, pl.ds(0, N1), pl.ds(0, rows)], r_recv.at[0]).wait_recv())
 
     def turned(w):
-        return parts(jnp.concatenate([w[:, cols(c)].T for c in range(3)], axis=0))
+        return jnp.concatenate([w[:, cols(c)].T for c in range(3)], axis=0)
 
     for i in range(8):
         w = jnp.concatenate(w_rows(i, range(N1)) + small_rows(i), axis=0)
         here = (kt < 0) | ((ks == 0) & (ku >> 1 == i % 4)) | ((ks > 0) & (ku >> 2 == i % 2))
         f1 = jnp.where(here, f1_mat[...], 0.0).astype(BF16)
-        v_acc[i] = dot(turned(w), jnp.concatenate([f1] * 3, axis=0))
+        v = dot(parts(turned(w)), jnp.concatenate([f1] * 3, axis=0))
+        for h in range(2):
+            v_acc[h, i] = v[CH * h:CH * h + CH]
+
+    across = pltpu.make_async_remote_copy(
+        src_ref=v_acc.at[1 - core], dst_ref=v_in, send_sem=v_sem.at[0], recv_sem=v_sem.at[1],
+        device_id=partner, device_id_type=MESH)
+    across.start()
 
     for m, (_, nq) in enumerate(SMALL):
-        all_of(ps_s.at[m, :, pl.ds(0, 24 * nq)], ds_sem.at[0, m]).wait_send()
+        all_of(ps_s.at[m, :, pl.ds(0, 24 * nq)], ds_send.at[m]).wait_send()
         all_of(own_s.at[m, pl.ds(0, 3), pl.ds(0, 24 * nq)], rs_send.at[m]).wait_send()
     all_of(ps_m, d_send).wait_send()
     by_core(lambda rows: all_of(rb_m.at[:, N1, pl.ds(0, rows)], r_recv.at[1]).wait_recv())
 
-    def back(i):
-        return pltpu.make_async_remote_copy(
-            src_ref=v_fin.at[i], dst_ref=out_ref.at[core * 8 + i], send_sem=v_sem.at[0], recv_sem=v_sem.at[1],
-            device_id=partner, device_id_type=MESH)
-
     rows = [v for i in range(7) for v in w_rows(i, range(N1, NM))]
     rows += [jnp.where(core == 0, v, 0.0) for v in w_rows(7, range(N1, NM))]
-    w = turned(jnp.concatenate(rows, axis=0))
-    vs = [dot(w, f2_mat[:, cols(2 * g, 2)]) for g in range(4)]
-    for g, v in enumerate(vs):
-        for i in (2 * g, 2 * g + 1):
-            vi = v_acc[i] + v[:, cols(i % 2)]
-            low, high = vi[0:NC, 0:NV], vi[CH:CH + NC, 0:NV]
-            v_fin[i] = jnp.where(core == 0, high, low)
-            if i < 7:
-                out_ref[core * 8 + i] = jnp.where(core == 0, low, high)
-            else:
-                @pl.when(core == 0)
-                def _():
-                    out_ref[7] = low
-        if g % 2:
-            for i in range(2 * g - 2, 2 * g + 2):
-                if i < 7:
-                    back(i).start()
-                else:
-                    @pl.when(core == 0)
-                    def _():
-                        back(7).start()
-
-    def close(rows):
-        n = 8 if rows == RW else 7
-        all_of(own_m.at[:, pl.ds(0, 3), pl.ds(0, rows)], r_send).wait_send()
-        all_of(v_fin.at[pl.ds(0, n)], v_sem.at[0]).wait_send()
-        all_of(out_ref.at[pl.ds(8 if n == 8 else 0, NO - n)], v_sem.at[1]).wait_recv()
-
-    by_core(close)
+    w2[...] = jnp.concatenate(rows, axis=0)
+    last = pltpu.make_async_remote_copy(
+        src_ref=w2, dst_ref=w2_in, send_sem=w_sem.at[0], recv_sem=w_sem.at[1], device_id=partner, device_id_type=MESH)
+    last.start()
+
+    def finish_v(w, acc, who):
+        t = turned(w)
+        t = parts(jnp.where(core == 0, t[0:CH], t[CH:2 * CH]))
+        vs = [dot(t, f2_mat[:, cols(2 * g, 2)]) for g in range(4)]
+        for i in range(7):
+            out_ref[who * 8 + i] = (acc(i) + vs[i // 2][:, cols(i % 2)])[0:NC, 0:NV]
+
+        @pl.when(who == 0)
+        def _():
+            out_ref[7] = (acc(7) + vs[3][:, cols(1)])[0:NC, 0:NV]
+
+    finish_v(w2[...], lambda i: v_acc[core, i], core)
+    across.wait_recv()
+    last.wait_recv()
+    finish_v(w2_in[...], lambda i: v_in[i], 1 - core)
+    across.wait_send()
+    last.wait_send()
+    by_core(lambda rows: all_of(own_m.at[:, pl.ds(0, 3), pl.ds(0, rows)], r_send).wait_send())
 
 
 def solution(mesh):
@@ -424,18 +424,22 @@
                 pltpu.VMEM((3, 4, 96, L), F32),
                 pltpu.VMEM((3, NM, RW, L), F32),
                 pltpu.VMEM((3, 3, 96, L), F32),
-                pltpu.VMEM((8, LW, L), F32),
-                pltpu.VMEM((8, NC, NV), F32),
+                pltpu.VMEM((2, 8, CH, L), F32),
+                pltpu.VMEM((8, CH, L), F32),
+                pltpu.VMEM((L, LW), F32),
+                pltpu.VMEM((L, LW), F32),
                 pltpu.SemaphoreType.DMA((2, 2)),
-                pltpu.SemaphoreType.DMA((3,)),
+                pltpu.SemaphoreType.DMA((3, 2)),
                 pltpu.SemaphoreType.DMA((2,)),
                 pltpu.SemaphoreType.DMA,
                 pltpu.SemaphoreType.DMA((NM, 2)),
-                pltpu.SemaphoreType.DMA((2, 3)),
+                pltpu.SemaphoreType.DMA((3,)),
+                pltpu.SemaphoreType.DMA((3, 2)),
                 pltpu.SemaphoreType.DMA,
                 pltpu.SemaphoreType.DMA((2,)),
                 pltpu.SemaphoreType.DMA((3,)),
                 pltpu.SemaphoreType.DMA((3,)),
+                pltpu.SemaphoreType.DMA((2,)),
                 pltpu.SemaphoreType.DMA((2,)),
             ],
             compiler_params=pltpu.CompilerParams(

time: 41.4 us -> 40.2 us (0.971)
  Pallas kernels: 40.2 us -> 39 us
    pallas_call x1, Pallas kernels: 40.2 us -> 39 us  [local_program(): pl.pallas_call(kernel, out_shape=pltpu.VMEM((NO, NC, NV), F32), in_specs=...]
where the time goes in v8:
time: 40.2 us; the launch traced here: 40.1 us
  Pallas kernels  39 us (97%)
  local copies, waits for them, and re-layouts  1.09 us (3%)
    pallas_call x1, Pallas kernels, local_program(): pl.pallas_call(kernel, out_shape=pltpu.VMEM((NO, NC, NV), F32), in_specs=...  39 us
    unnamed x1, local copies, waits for them, and re-layouts  1.09 us

profile of v8, /device:TPU:0, one launch (start us, length us, event | category | flops | bytes accessed | tf_op | source)
XLA Modules:
  0.0 40.1 jit_solution(6203093228247208012)
XLA Ops:
  0.0 39.0 %four_index.1 = f32[15,180,96]{2,1,0:T(8,128)S(1)} custom-call(bf16[29,58,116,116]{3,2,1,0:T(8,128)(2,1)} %a_hbm.1, bf16[15,116]{1,0:T(8,128)(2,1)} %bitcast.5, bf16[96,116]{1,0:T(8,128)(2,1)} %bitcast.4), custom_call_target="tpu_custom_call" | custom-call | tf_op jit(solution)/shard_map/four_index/pallas_call | solution.py:395
  39.0 1.1 %copy.5 = f32[15,96,180]{1,2,0:T(8,128)} copy(f32[15,96,180]{1,2,0:T(8,128)S(1)} %bitcast.3) | data formatting | bytes 2073600

commit v9 on v8

--- a/solution.py
+++ b/solution.py
@@ -101,19 +101,29 @@
     cv = cvt[...].T.astype(BF16)
     first = [(15 * c) // 4 for c in chip]
     first_s = [4 * c + 2 - c // 3 for c in chip]
-    lane, row = iota((L, 256), 1), iota((L, 256), 0)
-    want = jnp.where(lane < NC, lane, jnp.where(lane < CH, -100000, lane - 4)) - row
-    lane_s, row_s = iota((L, L), 1), iota((L, L), 0)
-    want_s = jnp.where(lane_s < SP, lane_s + 252, -100000) - row_s
+    lane, row = iota((1, 256), 1), iota((L, 256), 0)
     bs_mat[...] = jnp.zeros_like(bs_mat)
+
+    def full_of(rel, block, j0, steps):
+        c = rel + 360 * block
+        step = sum((c >= 96 * (j0 + t)).astype(I32) for t in range(1, steps))
+        place = jnp.where(row == c - 96 * (j0 + step), 1.0, 0.0).astype(BF16)
+        return dot(cv, place), step
+
+    far = -100000
+    rel = jnp.where(lane < NC, lane, jnp.where(lane < CH, far, lane - 4))
     for r in range(4):
-        for j in range(4):
-            place = jnp.where(want == 96 * (first[r] + j) - 360 * chip[r], 1.0, 0.0).astype(BF16)
-            b_mat[r, cols(j), :] = dot(cv, place).astype(BF16)
-        for j in range(2):
-            place = jnp.where(want_s == 96 * (first_s[r] + j) - 360 * chip[r], 1.0, 0.0).astype(BF16)
-            h = r % 2
-            bs_mat[r // 2, cols(2 * h + j), cols(h)] = dot(cv, place).astype(BF16)
+        full, step = full_of(rel, chip[r], first[r], 4)
+        for t in range(4):
+            b_mat[r, cols(t), :] = jnp.where(step == t, full, 0.0).astype(BF16)
+    rel = jnp.where((lane & (L - 1)) < SP, (lane & (L - 1)) + 252, far)
+    for p in range(2):
+        r0, r1 = 2 * p, 2 * p + 1
+        full, step = full_of(rel, jnp.where(lane < L, chip[r0], chip[r1]), jnp.where(lane < L, first_s[r0], first_s[r1]), 2)
+        for t in range(2):
+            some = jnp.where(step == t, full, 0.0).astype(BF16)
+            for h in range(2):
+                bs_mat[p, cols(2 * h + t), cols(h)] = some[:, cols(h)]
     low, high = cot[0:8, :], cot[8:16, :]
     mine = jnp.concatenate([jnp.where(core == 0, low, high), jnp.where(core == 0, high, low)], axis=0)
     kk = iota((L, 256), 1)
@@ -129,6 +139,8 @@
         l_mat[...] = jnp.where(here, dot(e, l0), 0.0).astype(BF16)
 
     build_l(l2, 1)
+    build_l(l4, 2)
+    build_l(l8, 3)
 
     def step1(tile_of, qp):
         zl = jnp.zeros((NB, L - NB), BF16)
@@ -221,16 +233,18 @@
             if r < 3:
                 out_s(m, r).start()
 
-    for c in small_copy[2]:
-        c.start()
     for m, (l_mat, a_ref) in enumerate(zip((l2, l4, l4), a_small)):
         nq = SMALL[m][1]
         for qp in range(nq // 2):
             small_copy[m][qp].wait()
             step1(lambda p, q: a_ref[p, 2 * qp + q], qp)
         if m == 0:
+            for c in small_copy[2]:
+                c.start()
             pl.semaphore_wait(barrier, 4)
         else:
+            for half in range(2):
+                a_copy(m - 1, half, m - 1).start()
             finish_s(m - 1)
         rows = 32 * nq
         for k in range(6):
@@ -243,12 +257,6 @@
                     ps_s[m, r, rows8(c * nq, nq), :] = w[rows8(nq, nq), cols(c)]
             for r in pair:
                 d2d_s(m, r).start()
-        if m < 2:
-            for half in range(2):
-                a_copy(m, half, m).start()
-        if m == 0:
-            build_l(l4, 2)
-            build_l(l8, 3)
 
     def body(n, carry):
         slot = lax.rem(n, 2)
@@ -365,14 +373,16 @@
 
     rows = [v for i in range(7) for v in w_rows(i, range(N1, NM))]
     rows += [jnp.where(core == 0, v, 0.0) for v in w_rows(7, range(N1, NM))]
-    w2[...] = jnp.concatenate(rows, axis=0)
+    w = jnp.concatenate(rows, axis=0)
+    for c in range(3):
+        w2[c] = w[:, cols(c)]
     last = pltpu.make_async_remote_copy(
-        src_ref=w2, dst_ref=w2_in, send_sem=w_sem.at[0], recv_sem=w_sem.at[1], device_id=partner, device_id_type=MESH)
+        src_ref=w2.at[pl.ds(1 - core, 2)], dst_ref=w2_in, send_sem=w_sem.at[0], recv_sem=w_sem.at[1], device_id=partner, device_id_type=MESH)
     last.start()
 
     def finish_v(w, acc, who):
-        t = turned(w)
-        t = parts(jnp.where(core == 0, t[0:CH], t[CH:2 * CH]))
+        t = jnp.concatenate([v.T for v in w], axis=0)
+        t = parts(jnp.where(core == 0, t[0:CH], t[CH - L:2 * CH - L]))
         vs = [dot(t, f2_mat[:, cols(2 * g, 2)]) for g in range(4)]
         for i in range(7):
             out_ref[who * 8 + i] = (acc(i) + vs[i // 2][:, cols(i % 2)])[0:NC, 0:NV]
@@ -381,10 +391,10 @@
         def _():
             out_ref[7] = (acc(7) + vs[3][:, cols(1)])[0:NC, 0:NV]
 
-    finish_v(w2[...], lambda i: v_acc[core, i], core)
+    finish_v([w2[core], w2[core + 1]], lambda i: v_acc[core, i], core)
     across.wait_recv()
     last.wait_recv()
-    finish_v(w2_in[...], lambda i: v_in[i], 1 - core)
+    finish_v([w2_in[0], w2_in[1]], lambda i: v_in[i], 1 - core)
     across.wait_send()
     last.wait_send()
     by_core(lambda rows: all_of(own_m.at[:, pl.ds(0, 3), pl.ds(0, rows)], r_send).wait_send())
@@ -426,8 +436,8 @@
                 pltpu.VMEM((3, 3, 96, L), F32),
                 pltpu.VMEM((2, 8, CH, L), F32),
                 pltpu.VMEM((8, CH, L), F32),
-                pltpu.VMEM((L, LW), F32),
-                pltpu.VMEM((L, LW), F32),
+                pltpu.VMEM((3, L, L), F32),
+                pltpu.VMEM((2, L, L), F32),
                 pltpu.SemaphoreType.DMA((2, 2)),
                 pltpu.SemaphoreType.DMA((3, 2)),
                 pltpu.SemaphoreType.DMA((2,)),

time: 40.2 us -> 39.8 us (0.990)
    pallas_call x1, Pallas kernels: 39 us -> 38.6 us  [local_program(): pl.pallas_call(kernel, out_shape=pltpu.VMEM((NO, NC, NV), F32), in_specs=...]
where the time goes in v9:
time: 39.8 us; the launch traced here: 39.7 us
  Pallas kernels  38.6 us (97%)
  local copies, waits for them, and re-layouts  1.09 us (3%)
    pallas_call x1, Pallas kernels, local_program(): pl.pallas_call(kernel, out_shape=pltpu.VMEM((NO, NC, NV), F32), in_specs=...  38.6 us
    unnamed x1, local copies, waits for them, and re-layouts  1.09 us

profile of v9, /device:TPU:0, one launch (start us, length us, event | category | flops | bytes accessed | tf_op | source)
XLA Modules:
  0.0 39.7 jit_solution(263906286370492315)
XLA Ops:
  0.0 38.6 %four_index.1 = f32[15,180,96]{2,1,0:T(8,128)S(1)} custom-call(bf16[29,58,116,116]{3,2,1,0:T(8,128)(2,1)} %a_hbm.1, bf16[15,116]{1,0:T(8,128)(2,1)} %bitcast.5, bf16[96,116]{1,0:T(8,128)(2,1)} %bitcast.4), custom_call_target="tpu_custom_call" | custom-call | tf_op jit(solution)/shard_map/four_index/pallas_call | solution.py:405
  38.6 1.1 %copy.5 = f32[15,96,180]{1,2,0:T(8,128)} copy(f32[15,96,180]{1,2,0:T(8,128)S(1)} %bitcast.3) | data formatting | bytes 2073600

commit v10 on v9

--- a/solution.py
+++ b/solution.py
@@ -60,8 +60,8 @@
     core = lax.rem(dev, 2)
     x = dev // 2
     partner = (0, y, x * 2 + (1 - core))
-    peers = [(0, 1 - y, (1 - x) * 2 + core), (0, y, (1 - x) * 2 + core), (0, 1 - y, x * 2 + core)]
-    chip = [2 * (1 - y) + (1 - x), 2 * y + (1 - x), 2 * (1 - y) + x, 2 * y + x]
+    peers = [(0, 1 - y, (1 - x) * 2 + core), (0, 1 - y, x * 2 + core), (0, y, (1 - x) * 2 + core)]
+    chip = [2 * (1 - y) + (1 - x), 2 * (1 - y) + x, 2 * y + (1 - x), 2 * y + x]
 
     def a_copy(n, half, slot):
         return pltpu.make_async_copy(
@@ -296,8 +296,8 @@
 
     def w_rows(i, ns):
         def block(n, b):
-            near = own_m[n, 3, rows8(b), :] + rb_m[1, n, rows8(b), :]
-            far = rb_m[2, n, rows8(b), :] + rb_m[0, n, rows8(b), :]
+            near = own_m[n, 3, rows8(b), :] + rb_m[2, n, rows8(b), :]
+            far = rb_m[1, n, rows8(b), :] + rb_m[0, n, rows8(b), :]
             return near, far
 
         both = []
@@ -319,8 +319,8 @@
             own, ins = [], []
             for c in range(3):
                 t = rows8(c * nq + (i * nq) // 8)
-                own.append(own_s[m, 3, t, :] + rb_s[1, m, t, :])
-                ins.append(rb_s[2, m, t, :] + rb_s[0, m, t, :])
+                own.append(own_s[m, 3, t, :] + rb_s[2, m, t, :])
+                ins.append(rb_s[1, m, t, :] + rb_s[0, m, t, :])
             out += [jnp.concatenate(own, axis=1), jnp.concatenate(ins, axis=1)]
         return out
 

time: 39.8 us -> 39.2 us (0.985)
  Pallas kernels: 38.6 us -> 38 us
    pallas_call x1, Pallas kernels: 38.6 us -> 38 us  [local_program(): pl.pallas_call(kernel, out_shape=pltpu.VMEM((NO, NC, NV), F32), in_specs=...]
where the time goes in v10:
time: 39.2 us; the launch traced here: 39.1 us
  Pallas kernels  38 us (97%)
  local copies, waits for them, and re-layouts  1.09 us (3%)
    pallas_call x1, Pallas kernels, local_program(): pl.pallas_call(kernel, out_shape=pltpu.VMEM((NO, NC, NV), F32), in_specs=...  38 us
    unnamed x1, local copies, waits for them, and re-layouts  1.09 us

profile of v10, /device:TPU:0, one launch (start us, length us, event | category | flops | bytes accessed | tf_op | source)
XLA Modules:
  0.0 39.1 jit_solution(10491913377724627860)
XLA Ops:
  0.0 38.0 %four_index.1 = f32[15,180,96]{2,1,0:T(8,128)S(1)} custom-call(bf16[29,58,116,116]{3,2,1,0:T(8,128)(2,1)} %a_hbm.1, bf16[15,116]{1,0:T(8,128)(2,1)} %bitcast.5, bf16[96,116]{1,0:T(8,128)(2,1)} %bitcast.4), custom_call_target="tpu_custom_call" | custom-call | tf_op jit(solution)/shard_map/four_index/pallas_call | solution.py:405
  38.0 1.1 %copy.5 = f32[15,96,180]{1,2,0:T(8,128)} copy(f32[15,96,180]{1,2,0:T(8,128)S(1)} %bitcast.3) | data formatting | bytes 2073600

commit v11 on v10

--- a/solution.py
+++ b/solution.py
@@ -186,13 +186,13 @@
 
     def d2d(n, r):
         return pltpu.make_async_remote_copy(
-            src_ref=ps_m.at[n, r], dst_ref=pr_m.at[n, r], send_sem=d_send, recv_sem=d_recv.at[n, r // 2],
+            src_ref=ps_m.at[n, r], dst_ref=pr_m.at[n, r], send_sem=d_send, recv_sem=d_recv.at[n % 2, r // 2],
             device_id=partner, device_id_type=MESH)
 
     def d2d_s(m, r):
         part = pl.ds(0, 24 * SMALL[m][1])
         return pltpu.make_async_remote_copy(
-            src_ref=ps_s.at[m, r, part], dst_ref=pr_s.at[m, r, part], send_sem=ds_send.at[m],
+            src_ref=ps_s.at[m, r, part], dst_ref=pr_s.at[m, r, part], send_sem=ds_send,
             recv_sem=ds_recv.at[m, r // 2], device_id=partner, device_id_type=MESH)
 
     def out_m(n, r, rows):
@@ -203,8 +203,8 @@
     def out_s(m, r):
         part = pl.ds(0, 24 * SMALL[m][1])
         return pltpu.make_async_remote_copy(
-            src_ref=own_s.at[m, r, part], dst_ref=rb_s.at[r, m, part], send_sem=rs_send.at[m],
-            recv_sem=rs_recv.at[m], device_id=peers[r], device_id_type=MESH)
+            src_ref=own_s.at[m, r, part], dst_ref=rb_s.at[r, m, part], send_sem=rs_send,
+            recv_sem=rs_recv, device_id=peers[r], device_id_type=MESH)
 
     def by_core(f):
         for k in range(2):
@@ -213,7 +213,7 @@
                 f(ROWS[k])
 
     def finish_m(n, rs):
-        all_of(pr_m.at[n, pl.ds(rs[0], 2)], d_recv.at[n, rs[0] // 2]).wait_recv()
+        all_of(pr_m.at[n, pl.ds(rs[0], 2)], d_recv.at[n % 2, rs[0] // 2]).wait_recv()
         for r in rs:
             own_m[n, r] = own_m[n, r] + pr_m[n, r]
 
@@ -345,8 +345,7 @@
         for k in range(3):
             f2_mat[cols(k), cols(i)] = mine_f
 
-    for m, (_, nq) in enumerate(SMALL):
-        all_of(rb_s.at[:, m, pl.ds(0, 24 * nq)], rs_recv.at[m]).wait_recv()
+    all_of(rb_s.at[:, :, pl.ds(0, 80)], rs_recv).wait_recv()
     by_core(lambda rows: all_of(rb_m.at[:, pl.ds(0, N1), pl.ds(0, rows)], r_recv.at[0]).wait_recv())
 
     def turned(w):
@@ -365,9 +364,8 @@
         device_id=partner, device_id_type=MESH)
     across.start()
 
-    for m, (_, nq) in enumerate(SMALL):
-        all_of(ps_s.at[m, :, pl.ds(0, 24 * nq)], ds_send.at[m]).wait_send()
-        all_of(own_s.at[m, pl.ds(0, 3), pl.ds(0, 24 * nq)], rs_send.at[m]).wait_send()
+    all_of(ps_s.at[:, :, pl.ds(0, 80)], ds_send).wait_send()
+    all_of(own_s.at[:, pl.ds(0, 3), pl.ds(0, 80)], rs_send).wait_send()
     all_of(ps_m, d_send).wait_send()
     by_core(lambda rows: all_of(rb_m.at[:, N1, pl.ds(0, rows)], r_recv.at[1]).wait_recv())
 
@@ -442,13 +440,13 @@
                 pltpu.SemaphoreType.DMA((3, 2)),
                 pltpu.SemaphoreType.DMA((2,)),
                 pltpu.SemaphoreType.DMA,
-                pltpu.SemaphoreType.DMA((NM, 2)),
-                pltpu.SemaphoreType.DMA((3,)),
+                pltpu.SemaphoreType.DMA((2, 2)),
+                pltpu.SemaphoreType.DMA,
                 pltpu.SemaphoreType.DMA((3, 2)),
                 pltpu.SemaphoreType.DMA,
                 pltpu.SemaphoreType.DMA((2,)),
-                pltpu.SemaphoreType.DMA((3,)),
-                pltpu.SemaphoreType.DMA((3,)),
+                pltpu.SemaphoreType.DMA,
+                pltpu.SemaphoreType.DMA,
                 pltpu.SemaphoreType.DMA((2,)),
                 pltpu.SemaphoreType.DMA((2,)),
             ],

time: 39.2 us -> 39.1 us (level)
  no operation moved by 1% of the time
where the time goes in v11:
time: 39.1 us; the launch traced here: 39 us
  Pallas kernels  37.9 us (97%)
  local copies, waits for them, and re-layouts  1.09 us (3%)
    pallas_call x1, Pallas kernels, local_program(): pl.pallas_call(kernel, out_shape=pltpu.VMEM((NO, NC, NV), F32), in_specs=...  37.9 us
    unnamed x1, local copies, waits for them, and re-layouts  1.09 us

profile of v11, /device:TPU:0, one launch (start us, length us, event | category | flops | bytes accessed | tf_op | source)
XLA Modules:
  0.0 39.0 jit_solution(7103393615279875556)
XLA Ops:
  0.0 37.9 %four_index.1 = f32[15,180,96]{2,1,0:T(8,128)S(1)} custom-call(bf16[29,58,116,116]{3,2,1,0:T(8,128)(2,1)} %a_hbm.1, bf16[15,116]{1,0:T(8,128)(2,1)} %bitcast.5, bf16[96,116]{1,0:T(8,128)(2,1)} %bitcast.4), custom_call_target="tpu_custom_call" | custom-call | tf_op jit(solution)/shard_map/four_index/pallas_call | solution.py:403
  37.9 1.1 %copy.5 = f32[15,96,180]{1,2,0:T(8,128)} copy(f32[15,96,180]{1,2,0:T(8,128)S(1)} %bitcast.3) | data formatting | bytes 2073600

commit v12 on v11

--- a/solution.py
+++ b/solution.py
@@ -74,7 +74,7 @@
     small = [pltpu.make_async_copy(cot_hbm, cot_in, c_sem.at[0]), pltpu.make_async_copy(cvt_hbm, cvt_in, c_sem.at[1])]
     a_small = (as0, as1, as2)
     small_copy = [[pltpu.make_async_copy(a_hbm.at[:, pl.ds(q + 2 * k, 2)], a_small[m].at[:, pl.ds(2 * k, 2)],
-                                         as_sem.at[m, k]) for k in range(nq // 2)]
+                                         as_sem.at[max(2 * m - 1, 0) + k]) for k in range(nq // 2)]
                   for m, (q, nq) in enumerate(SMALL)]
     for c in small:
         c.start()
@@ -193,7 +193,7 @@
         part = pl.ds(0, 24 * SMALL[m][1])
         return pltpu.make_async_remote_copy(
             src_ref=ps_s.at[m, r, part], dst_ref=pr_s.at[m, r, part], send_sem=ds_send,
-            recv_sem=ds_recv.at[m, r // 2], device_id=partner, device_id_type=MESH)
+            recv_sem=ds_recv.at[m % 2, r // 2], device_id=partner, device_id_type=MESH)
 
     def out_m(n, r, rows):
         return pltpu.make_async_remote_copy(
@@ -228,7 +228,7 @@
         part = rows8(0, 3 * SMALL[m][1])
         for r in range(4):
             if r % 2 == 0:
-                all_of(pr_s.at[m, pl.ds(r, 2), pl.ds(0, 24 * SMALL[m][1])], ds_recv.at[m, r // 2]).wait_recv()
+                all_of(pr_s.at[m, pl.ds(r, 2), pl.ds(0, 24 * SMALL[m][1])], ds_recv.at[m % 2, r // 2]).wait_recv()
             own_s[m, r, part, :] = own_s[m, r, part, :] + pr_s[m, r, part, :]
             if r < 3:
                 out_s(m, r).start()
@@ -437,12 +437,12 @@
                 pltpu.VMEM((3, L, L), F32),
                 pltpu.VMEM((2, L, L), F32),
                 pltpu.SemaphoreType.DMA((2, 2)),
-                pltpu.SemaphoreType.DMA((3, 2)),
+                pltpu.SemaphoreType.DMA((5,)),
                 pltpu.SemaphoreType.DMA((2,)),
                 pltpu.SemaphoreType.DMA,
                 pltpu.SemaphoreType.DMA((2, 2)),
                 pltpu.SemaphoreType.DMA,
-                pltpu.SemaphoreType.DMA((3, 2)),
+                pltpu.SemaphoreType.DMA((2, 2)),
                 pltpu.SemaphoreType.DMA,
                 pltpu.SemaphoreType.DMA((2,)),
                 pltpu.SemaphoreType.DMA,

time: 39.1 us -> 39.1 us (level)
  no operation moved by 1% of the time
where the time goes in v12:
time: 39.1 us; the launch traced here: 39 us
  Pallas kernels  37.8 us (97%)
  local copies, waits for them, and re-layouts  1.09 us (3%)
    pallas_call x1, Pallas kernels, local_program(): pl.pallas_call(kernel, out_shape=pltpu.VMEM((NO, NC, NV), F32), in_specs=...  37.8 us
    unnamed x1, local copies, waits for them, and re-layouts  1.09 us

profile of v12, /device:TPU:0, one launch (start us, length us, event | category | flops | bytes accessed | tf_op | source)
XLA Modules:
  0.0 39.0 jit_solution(9384237775440447218)
XLA Ops:
  0.0 37.8 %four_index.1 = f32[15,180,96]{2,1,0:T(8,128)S(1)} custom-call(bf16[29,58,116,116]{3,2,1,0:T(8,128)(2,1)} %a_hbm.1, bf16[15,116]{1,0:T(8,128)(2,1)} %bitcast.5, bf16[96,116]{1,0:T(8,128)(2,1)} %bitcast.4), custom_call_target="tpu_custom_call" | custom-call | tf_op jit(solution)/shard_map/four_index/pallas_call | solution.py:403
  37.9 1.1 %copy.5 = f32[15,96,180]{1,2,0:T(8,128)} copy(f32[15,96,180]{1,2,0:T(8,128)S(1)} %bitcast.3) | data formatting | bytes 2073600
